TPU v7x, 32 devices: a whole 2x2x4 slice. The times are simulated.
32 devices in a mesh: group: 4 (over y, x), dev: 8 (over z, core).
Axes of the slice: x: 2, y: 2, z: 4, core: 2. Of those that a mesh axis runs over, the one named last changes fastest.
Arguments:
- grid_state: bfloat16 [32768, 512], P(('group', 'dev')), may hold values from -6 to 6
- mesh_state: bfloat16 [4096, 512], P(('group', 'dev')), may hold values from -6 to 6
- encode_edge: bfloat16 [512, 512], replicated, may hold values from -0.25 to 0.25
- encode_first: bfloat16 [512, 512], replicated, may hold values from -0.25 to 0.25
- encode_second: bfloat16 [512, 512], replicated, may hold values from -0.25 to 0.25
- process_edge: bfloat16 [512, 512], replicated, may hold values from -0.25 to 0.25
- process_first: bfloat16 [512, 512], replicated, may hold values from -0.25 to 0.25
- process_second: bfloat16 [512, 512], replicated, may hold values from -0.25 to 0.25
- decode_edge: bfloat16 [512, 512], replicated, may hold values from -0.25 to 0.25
- decode_first: bfloat16 [512, 512], replicated, may hold values from -0.25 to 0.25
- decode_second: bfloat16 [512, 512], replicated, may hold values from -0.25 to 0.25
- encode_near: bfloat16 [3, 4096, 1024], P(None, ('group', 'dev')), may hold values from -0.09375 to 0.09375
- encode_live: int32 [3, 256], P(None, ('group', 'dev')), may hold values 0 or 1
- encode_far: bfloat16 [2, 4096, 1024], P(None, ('group', 'dev')), may hold values from -0.09375 to 0.09375
- encode_groups: int32 [2, 32], P(None, ('group', 'dev')), may hold values from 0 to 3, as said below
- process_near: bfloat16 [3, 4096, 128], P(None, ('group', 'dev')), may hold values from -0.25 to 0.25
- process_far: bfloat16 [2, 4096, 128], P(None, ('group', 'dev')), may hold values from -0.25 to 0.25
- process_groups: int32 [2, 32], P(None, ('group', 'dev')), may hold values from 0 to 3, as said below
- decode_near: bfloat16 [3, 32768, 128], P(None, ('group', 'dev')), may hold values from -0.3125 to 0.3125
- decode_live: int32 [3, 256], P(None, ('group', 'dev')), may hold values 0 or 1
Outputs:
- grid_next: bfloat16 [32768, 512], P(('group', 'dev'))
- mesh_next: bfloat16 [4096, 512], P(('group', 'dev'))
Inputs may be any that keep to these rules, and one draw needn't show every extreme that they name: `encode_groups`: for each device q the 2 entries of column q are distinct regions, none equal to q's own region q // 8. `process_groups`: for each device q the 2 entries of column q are distinct regions, none equal to q's own region q // 8.
All inputs are finite; a program needn't handle non-finite values. No bound on the sum of `encode_live` or of `decode_live` on one device may be relied on, other than what follows from the above.
Results may differ from a plain program's by a relative error of at most 0.013.
Values may be sent and summed in bfloat16 or wider, within the bound.
A program may use at most 64 MiB of HBM per device.

v0:
```python
import functools

import jax
import jax.numpy as jnp
from jax import lax
from jax.experimental import pallas as pl
from jax.experimental.pallas import tpu as pltpu
from jax.sharding import PartitionSpec as P

BF16 = jnp.bfloat16
F32 = jnp.float32
CHUNKS = 2


def silu(x):
    half = 0.5 * x
    return half + half * jnp.tanh(half)


def mm(a, b):
    return jnp.dot(a, b, preferred_element_type=F32)


def layer_norm(v):
    mean = jnp.mean(v, axis=-1, keepdims=True)
    cent = v - mean
    var = jnp.mean(cent * cent, axis=-1, keepdims=True)
    return cent * lax.rsqrt(var + 1e-05)


def partner(me, r, count):
    if count & (count - 1):
        return lax.rem(me + r, count), lax.rem(me + count - r, count)
    out, bit = me, 1
    while bit < count:
        if r & bit:
            out = out + bit * (1 - 2 * lax.rem(me // bit, 2))
        bit *= 2
    return out, out


def kernel(
    groups,
    devs,
    grid_h, mesh_h, ee_h, e1_h, e2_h, pe_h, p1_h, p2_h, de_h, d1_h, d2_h,
    en_h, el_h, ef_h, eg_h, pn_h, pf_h, pg_h, dn_h, dl_h,
    grid_o, mesh_o,
    gs, ms, wt, inc, el, eg, pn, pf, pg, dn, dl,
    em, fheld, fsend, frecv, nsend, nrecv, msend, mfrecv, mnrecv, dsend, dnrecv,
    own_near, proc_inc, dec_own, mesh_out, grid_out,
    load_sem, grid_sem, fs_sem, fr_sem, ns_sem, nr_sem, mfs_sem, mfr_sem, mns_sem, mnr_sem, ds_sem, dr_sem, out_sem,
):
    g = lax.axis_index("group")
    d = lax.axis_index("dev")
    rows, feats = ms.shape
    width = feats // CHUNKS
    far_count = groups - 1
    long_count = pf.shape[0]
    tiles = el.shape[1]
    peers = [partner(g, r, groups) for r in range(1, groups)]
    order = list(reversed(range(far_count)))
    relay = groups == 4
    halves = fsend.shape[1]
    piece_rows = rows // halves
    if relay:
        greeted = [to for to, _ in peers[:2]]
    elif groups & (groups - 1):
        greeted = [to for to, _ in peers] + [source for _, source in peers]
    else:
        greeted = [to for to, _ in peers]
    not_first, not_last = d > 0, d < devs - 1
    sides = ((not_first, d - 1), (not_last, d + 1))

    def load(index, src, dst):
        return pltpu.make_async_copy(src, dst, load_sem.at[index])

    loads = [
        load(0, ee_h, wt.at[0]), load(2, eg_h, eg), load(3, ef_h, inc.at[pl.ds(0, long_count)]),
        load(4, el_h, el), load(5, en_h, inc.at[pl.ds(long_count, 3)]),
        load(6, mesh_h, ms), load(7, e1_h, wt.at[1]), load(8, e2_h, wt.at[2]), load(9, pe_h, wt.at[3]),
        load(10, pg_h, pg), load(11, pn_h, pn), load(12, pf_h, pf), load(13, p1_h, wt.at[4]), load(14, p2_h, wt.at[5]),
        load(15, de_h, wt.at[6]), load(16, dl_h, dl), load(17, dn_h, dn), load(18, d1_h, wt.at[7]), load(19, d2_h, wt.at[8]),
    ]
    step = 2 * rows
    count = gs.shape[0] // step
    grid_loads = [
        pltpu.make_async_copy(grid_h.at[pl.ds(i * step, step)], gs.at[pl.ds(i * step, step)], grid_sem.at[i])
        for i in range(count)
    ]
    loads[0].start()
    for copy in grid_loads:
        copy.start()
    for copy in loads[1:3]:
        copy.start()

    barrier = pltpu.get_barrier_semaphore()
    for to in greeted:
        pl.semaphore_signal(barrier, inc=1, device_id=(to, d), device_id_type=pl.DeviceIdType.MESH)
    for there, near in sides:
        @pl.when(there)
        def _():
            pl.semaphore_signal(barrier, inc=1, device_id=(g, near), device_id_type=pl.DeviceIdType.MESH)

    for side, (there, _) in enumerate(sides):
        @pl.when(jnp.logical_not(there))
        def _():
            for buf in (nrecv, mnrecv, dnrecv):
                for c in range(CHUNKS):
                    buf[c, side] = jnp.zeros((rows, width), BF16)

    def remote(src, dst, send, recv, to):
        return pltpu.make_async_remote_copy(
            src_ref=src, dst_ref=dst, send_sem=send, recv_sem=recv, device_id=to, device_id_type=pl.DeviceIdType.MESH
        )

    def first_axis(h):
        return h % 2

    def far_copy(c, h, i):
        to = i
        if relay:
            to = first_axis(h) if i < 2 else 1 - first_axis(h)
        at = (c, h, i)
        return remote(fsend.at[at], frecv.at[at], fs_sem.at[at], fr_sem.at[at], (peers[to][0], d))

    def near_copy(c, s):
        return remote(nsend.at[c, s], nrecv.at[c, 1 - s], ns_sem.at[c, s], nr_sem.at[c, 1 - s], (g, sides[s][1]))

    def near_in(c, s):
        return remote(nsend.at[c, s], nrecv.at[c, s], ns_sem.at[c, s], nr_sem.at[c, s], (g, sides[s][1]))

    def mfar_copy(c, h, i):
        at = pl.ds(h * piece_rows, piece_rows)
        source, to = msend.at[c, at], i
        if relay and i == 2:
            source, to = mfrecv.at[c, first_axis(h), at], 1 - first_axis(h)
        return remote(source, mfrecv.at[c, i, at], mfs_sem.at[c, h, i], mfr_sem.at[c, h, i], (peers[to][0], d))

    def mnear_copy(c, s):
        return remote(msend.at[c], mnrecv.at[c, 1 - s], mns_sem.at[c, s], mnr_sem.at[c, 1 - s], (g, sides[s][1]))

    def mnear_in(c, s):
        return remote(msend.at[c], mnrecv.at[c, s], mns_sem.at[c, s], mnr_sem.at[c, s], (g, sides[s][1]))

    def dec_copy(c, s):
        return remote(dsend.at[c], dnrecv.at[c, 1 - s], ds_sem.at[c, s], dr_sem.at[c, 1 - s], (g, sides[s][1]))

    def dec_in(c, s):
        return remote(dsend.at[c], dnrecv.at[c, s], ds_sem.at[c, s], dr_sem.at[c, s], (g, sides[s][1]))

    def start_side(copy, c):
        for s, (there, _) in enumerate(sides):
            @pl.when(there)
            def _():
                copy(c, s).start()

    def wait_side(copy, c, s):
        @pl.when(sides[s][0])
        def _():
            copy(c, s).wait_recv()

    loads[0].wait()
    for c in range(CHUNKS):
        cols = pl.ds(c * width, width)
        for i in range(count):
            if c == 0:
                grid_loads[i].wait()
            at = pl.ds(i * step, step)
            em[c, at, :] = silu(mm(gs[at, :], wt[0, :, cols])).astype(BF16)
        if c == 0:
            for copy in loads[3:]:
                copy.start()
            for copy in loads[1:3]:
                copy.wait()
        far = [mm(inc[i], em[c]) for i in range(long_count)]

        def toward(i):
            total = None
            for index in range(long_count):
                flag = jnp.where(eg[0, index] == peers[i][0], 1.0, 0.0).astype(F32)
                term = far[index] * flag
                total = term if total is None else total + term
            return total

        if c == 0:
            pl.semaphore_wait(barrier, len(greeted) + jnp.where(not_first, 1, 0) + jnp.where(not_last, 1, 0))
        if relay:
            totals = [toward(i) for i in range(far_count)]
            for kind in range(2):
                for h in range(halves):
                    at = slice(h * piece_rows, (h + 1) * piece_rows)
                    axis = first_axis(h)
                    fsend[c, h, kind] = totals[2 if kind == 0 else axis][at].astype(BF16)
                    far_copy(c, h, kind).start()
                    if kind == 0:
                        fheld[c, h] = totals[1 - axis][at]
        else:
            for i in order:
                fsend[c, 0, i] = toward(i).astype(BF16)
                far_copy(c, 0, i).start()
        if c == 0:
            for copy in loads[3:5]:
                copy.wait()
            for k in range(3):
                for t in range(tiles):
                    flag = el[k, t].astype(F32).astype(BF16)
                    at = pl.ds(t * rows, rows)
                    inc[long_count + k, :, at] = inc[long_count + k, :, at] * flag
        for s, k in ((0, 0), (1, 2)):
            nsend[c, s] = mm(inc[long_count + k], em[c]).astype(BF16)
        start_side(near_copy, c)
        own_near[:, cols] = mm(inc[long_count + 1], em[c]).astype(BF16)

    if relay:
        for c in range(CHUNKS):
            for h in range(halves):
                far_copy(c, h, 0).wait_recv()
                fsend[c, h, 2] = (fheld[c, h] + frecv[c, h, 0].astype(F32)).astype(BF16)
                far_copy(c, h, 2).start()

    for copy in loads[5:17]:
        copy.wait()
    for i in range(far_count):
        total = None
        for index in range(long_count):
            flag = jnp.where(pg[0, index] == peers[i][1], 1.0, 0.0).astype(F32)
            term = pf[index].astype(F32) * flag
            total = term if total is None else total + term
        proc_inc[i] = total.astype(BF16)
    for k in range(3):
        for t in range(tiles):
            at = pl.ds(t * rows, rows)
            dn[k, at, :] = dn[k, at, :] * dl[k, t].astype(F32).astype(BF16)

    for copy in loads[17:]:
        copy.wait()

    def node_update(residual, summed, first, second):
        hidden = silu(mm(layer_norm(summed).astype(BF16), wt[first])).astype(BF16)
        return (residual.astype(F32) + mm(hidden, wt[second])).astype(BF16)

    parts = []
    for c in range(CHUNKS):
        total = own_near[:, pl.ds(c * width, width)].astype(F32)
        for s in range(2):
            wait_side(near_in, c, s)
            total = total + nrecv[c, s].astype(F32)
        pieces = []
        for h in range(halves):
            piece = total[h * piece_rows:(h + 1) * piece_rows]
            for i in (1, 2) if relay else order:
                far_copy(c, h, i).wait_recv()
                piece = piece + frecv[c, h, i].astype(F32)
            pieces.append(piece)
        parts.append(jnp.concatenate(pieces, axis=0))
    mesh_mid = node_update(ms[...], jnp.concatenate(parts, axis=1), 1, 2)

    for c in range(CHUNKS):
        msend[c] = silu(mm(mesh_mid, wt[3, :, pl.ds(c * width, width)])).astype(BF16)
        if not relay:
            for i in order:
                mfar_copy(c, 0, i).start()
        else:
            for h in range(halves):
                mfar_copy(c, h, first_axis(h)).start()
        start_side(mnear_copy, c)
    if relay:
        for c in range(CHUNKS):
            for h in range(halves):
                mfar_copy(c, h, 1 - first_axis(h)).start()
    parts = [mm(pn[1], msend[c]) for c in range(CHUNKS)]
    if relay:
        for c in range(CHUNKS):
            for h in range(halves):
                mfar_copy(c, h, first_axis(h)).wait_recv()
                mfar_copy(c, h, 2).start()
    for c in range(CHUNKS):
        for s in range(2):
            wait_side(mnear_in, c, s)
            parts[c] = parts[c] + mm(pn[2 * s], mnrecv[c, s])
    for i in range(far_count) if relay else order:
        for c in range(CHUNKS):
            for h in range(halves):
                if not relay or i != first_axis(h):
                    mfar_copy(c, h, i).wait_recv()
            parts[c] = parts[c] + mm(proc_inc[i], mfrecv[c, i])
    mesh_next = node_update(mesh_mid, jnp.concatenate(parts, axis=1), 4, 5)
    mesh_out[...] = mesh_next

    for c in range(CHUNKS):
        dsend[c] = silu(mm(mesh_next, wt[6, :, pl.ds(c * width, width)])).astype(BF16)
        start_side(dec_copy, c)
    mesh_copy = pltpu.make_async_copy(mesh_out, mesh_o, out_sem.at[0])
    mesh_copy.start()

    def own_part(i, carry):
        at = pl.ds(pl.multiple_of(i * step, step), step)
        for c in range(CHUNKS):
            dec_own[at, pl.ds(c * width, width)] = mm(dn[1, at, :], dsend[c])
        return carry

    lax.fori_loop(0, count, own_part, 0)
    for c in range(CHUNKS):
        for s in range(2):
            wait_side(dec_in, c, s)
    outs = []
    for i in range(count):
        at = pl.ds(i * step, step)
        sums = []
        for c in range(CHUNKS):
            total = dec_own[at, pl.ds(c * width, width)]
            for s in range(2):
                total = total + mm(dn[2 * s, at, :], dnrecv[c, s])
            sums.append(total)
        grid_out[at, :] = node_update(gs[at, :], jnp.concatenate(sums, axis=1), 7, 8)
        copy = pltpu.make_async_copy(grid_out.at[at], grid_o.at[at], out_sem.at[1 + i])
        copy.start()
        outs.append(copy)

    for c in range(CHUNKS):
        for i in range(far_count):
            for h in range(halves):
                far_copy(c, h, i).wait_send()
                mfar_copy(c, h, i).wait_send()
        for s, (there, _) in enumerate(sides):
            @pl.when(there)
            def _():
                near_copy(c, s).wait_send()
                mnear_copy(c, s).wait_send()
                dec_copy(c, s).wait_send()
    mesh_copy.wait()
    for copy in outs:
        copy.wait()


def body(groups, devs, *args):
    grid_state, mesh_state = args[0], args[1]
    args = list(args)
    args[14], args[17] = args[14].T, args[17].T
    encode_live, encode_far, encode_groups = args[12], args[13], args[14]
    process_far, process_groups, decode_near, decode_live = args[16], args[17], args[18], args[19]
    grid_rows, feats = grid_state.shape
    rows = mesh_state.shape[0]
    width = feats // CHUNKS
    far_count = groups - 1
    long_count = encode_far.shape[0]

    def vmem(*shape, dtype=BF16):
        return pltpu.VMEM(shape, dtype)

    dma = pltpu.SemaphoreType.DMA
    halves = 2 if groups == 4 else 1
    pieces = (CHUNKS, halves, far_count)
    piece = (rows // halves, width)
    block = (rows, width)
    scratch = [
        vmem(grid_rows, feats), vmem(rows, feats), vmem(9, feats, feats), vmem(3 + long_count, rows, grid_rows),
        pltpu.SMEM(encode_live.shape, jnp.int32), pltpu.SMEM(encode_groups.shape, jnp.int32),
        vmem(3, rows, rows), vmem(*process_far.shape), pltpu.SMEM(process_groups.shape, jnp.int32),
        vmem(*decode_near.shape), pltpu.SMEM(decode_live.shape, jnp.int32),
        vmem(CHUNKS, grid_rows, width),
        vmem(CHUNKS, halves, *piece, dtype=F32), vmem(*pieces, *piece), vmem(*pieces, *piece),
        vmem(CHUNKS, 2, *block), vmem(CHUNKS, 2, *block),
        vmem(CHUNKS, *block), vmem(CHUNKS, far_count, *block), vmem(CHUNKS, 2, *block),
        vmem(CHUNKS, *block), vmem(CHUNKS, 2, *block),
        vmem(rows, feats), vmem(far_count, rows, rows), vmem(grid_rows, feats, dtype=F32), vmem(rows, feats),
        vmem(grid_rows, feats),
        dma((20,)), dma((grid_rows // (2 * rows),)), dma(pieces), dma(pieces), dma((CHUNKS, 2)), dma((CHUNKS, 2)),
        dma(pieces), dma(pieces), dma((CHUNKS, 2)), dma((CHUNKS, 2)),
        dma((CHUNKS, 2)), dma((CHUNKS, 2)), dma((1 + grid_rows // (2 * rows),)),
    ]
    hbm = pl.BlockSpec(memory_space=pl.ANY)
    return pl.pallas_call(
        functools.partial(kernel, groups, devs),
        out_shape=(
            jax.ShapeDtypeStruct(grid_state.shape, BF16),
            jax.ShapeDtypeStruct(mesh_state.shape, BF16),
        ),
        in_specs=[hbm] * len(args),
        out_specs=(hbm, hbm),
        scratch_shapes=scratch,
        compiler_params=pltpu.CompilerParams(collective_id=0, has_side_effects=True),
        name="step",
    )(*args)


def solution(mesh):
    both = ("group", "dev")
    row, whole, second = P(both, None), P(), P(None, both, None)
    flags = P(None, both)
    return jax.shard_map(
        functools.partial(body, mesh.shape["group"], mesh.shape["dev"]),
        mesh=mesh,
        in_specs=(
            row, row, whole, whole, whole, whole, whole, whole, whole, whole, whole,
            second, flags, second, flags, second, second, flags, second, flags,
        ),
        out_specs=(row, row),
        check_vma=False,
    )
```

profile of v0, /device:TPU:1, one launch (start us, length us, event | category | flops | bytes accessed | tf_op | source)
XLA Modules:
  0.0 33.5 jit_solution(17144808322397515417)
XLA Ops:
  0.6 29.9 %step.1 = (bf16[1024,512]{1,0:T(8,128)(2,1)}, bf16[128,512]{1,0:T(8,128)(2,1)}) custom-call(bf16[1024,512]{1,0:T(8,128)(2,1)} %grid_h.1, bf16[128,512]{1,0:T(8,128)(2,1)} %mesh_h.1, bf16[512,512]{1,0:T(8,128)(2,1)} %ee_h.1, bf16[512,512]{1,0:T(8,128)(2,1)} %e1_h.1, bf16[512,512]{1,0:T(8,128)(2,1)} %e2_h.1, bf16[512,512]{1,0:T(8,128)(2,1)} %pe_h.1, ...), custom_call_target="tpu_custom_call" | custom-call | tf_op jit(solution)/shard_map/step/pallas_call | solution.py:373
  30.6 0.0 copy-start
  30.6 2.3 %copy.24 = bf16[1024,512]{1,0:T(8,128)(2,1)} copy(bf16[1024,512]{1,0:T(8,128)(2,1)} %get-tuple-element.4) | data formatting | bytes 2097152
  32.9 0.0 copy-done
  32.9 0.7 %copy.25 = bf16[128,512]{1,0:T(8,128)(2,1)} copy(bf16[128,512]{1,0:T(8,128)(2,1)S(1)} %copy-done) | data formatting | bytes 262144
Async XLA Ops:
  30.6 2.3 %copy-start = (bf16[128,512]{1,0:T(8,128)(2,1)S(1)}, bf16[128,512]{1,0:T(8,128)(2,1)}, u32[]{:S(2)}) copy-start(bf16[128,512]{1,0:T(8,128)(2,1)} %get-tuple-element.5) | copy-start | bytes 393220
where the time goes:
time: 33.7 us; the launch traced here: 33.5 us
  Pallas kernels  29.9 us (89%)
  local copies, waits for them, and re-layouts  2.96 us (9%)
  between operations  0.66 us (2%)
    pallas_call x1, Pallas kernels, body(): pl.pallas_call(functools.partial(kernel, groups, devs), out_shape=(jax.Sh...  29.9 us
    unnamed x4, local copies, waits for them, and re-layouts  2.96 us

commit v1 on v0

v1 whole, which is shorter than its diff:
```python
import contextlib
import functools

import jax
import jax.numpy as jnp
from jax import lax
from jax.experimental import pallas as pl
from jax.experimental.pallas import tpu as pltpu
from jax.sharding import PartitionSpec as P

BF16 = jnp.bfloat16
F32 = jnp.float32
CHUNKS = 2
GRID_LOADS = 2
GRID_OUTS = 4


def silu(x):
    half = 0.5 * x
    return half + half * jnp.tanh(half)


def mm(a, b):
    return jnp.dot(a, b, preferred_element_type=F32)


def layer_norm(v):
    mean = jnp.mean(v, axis=-1, keepdims=True)
    cent = v - mean
    var = jnp.mean(cent * cent, axis=-1, keepdims=True)
    return cent * lax.rsqrt(var + 1e-05)


def partner(me, r, count):
    if count & (count - 1):
        return lax.rem(me + r, count), lax.rem(me + count - r, count)
    out, bit = me, 1
    while bit < count:
        if r & bit:
            out = out + bit * (1 - 2 * lax.rem(me // bit, 2))
        bit *= 2
    return out, out


def scope(name):
    return contextlib.nullcontext()


def exchange(
    groups,
    devs,
    grid_h, mesh_h, ee_h, e1_h, e2_h, pe_h, p1_h, p2_h, de_h, d1_h, d2_h,
    en_h, el_h, ef_h, eg_h, pn_h, pf_h, pg_h, dn_h, dl_h,
    mesh_out, gs, dw, acc,
    ms, wt, inc, live, regions, pinc, dn,
    em, fheld, fsend, frelay, frecv, nsend, nrecv, msend, mfrecv, mnrecv, dsend, dnrecv,
    own_near, proc_inc,
    load_sem, grid_sem, fs_sem, fl_sem, fr_sem, ns_sem, nr_sem, mfs_sem, mfl_sem, mfr_sem, mns_sem, mnr_sem, ds_sem, dr_sem,
):
    g = lax.axis_index("group")
    d = lax.axis_index("dev")
    rows, feats = ms.shape
    width = feats // CHUNKS
    far_count = groups - 1
    long_count = pinc.shape[0] - 3
    tiles = live.shape[2]
    peers = [partner(g, r, groups) for r in range(1, groups)]
    order = list(reversed(range(far_count)))
    relay = groups == 4
    halves = fsend.shape[2]
    piece_rows = rows // halves
    if relay:
        greeted = [to for to, _ in peers[:2]]
    elif groups & (groups - 1):
        greeted = [to for to, _ in peers] + [source for _, source in peers]
    else:
        greeted = [to for to, _ in peers]
    not_first, not_last = d > 0, d < devs - 1
    sides = ((not_first, d - 1), (not_last, d + 1))
    near_side = 1 - lax.rem(d, 2)

    def load(index, pairs, whole):
        starts = [pltpu.make_async_copy(src, dst, load_sem.at[index]) for src, dst in pairs]
        return starts, pltpu.make_async_copy(whole, whole, load_sem.at[index])

    far_inc, near_inc = inc.at[pl.ds(0, long_count)], inc.at[pl.ds(long_count, 3)]
    first = load(0, [(ee_h, wt.at[0])], wt.at[0])
    far_load = load(1, [(ef_h, far_inc)], far_inc)
    near_load = load(2, [(en_h, near_inc)], near_inc)
    live_load = load(3, [(el_h, live.at[0]), (dl_h, live.at[1])], live)
    region_load = load(4, [(eg_h, regions.at[0]), (pg_h, regions.at[1])], regions)
    late = [
        load(5, [(mesh_h, ms)], ms),
        load(6, [(e1_h, wt.at[1]), (e2_h, wt.at[2]), (pe_h, wt.at[3])], wt.at[pl.ds(1, 3)]),
        load(7, [(pn_h, pinc.at[pl.ds(0, 3)]), (pf_h, pinc.at[pl.ds(3, long_count)])], pinc),
        load(8, [(dn_h, dn)], dn),
        load(9, [(p1_h, wt.at[4]), (p2_h, wt.at[5]), (de_h, wt.at[6])], wt.at[pl.ds(4, 3)]),
        load(10, [(d1_h, dw.at[0]), (d2_h, dw.at[1])], dw),
    ]

    def start_load(loads):
        for copy in loads[0]:
            copy.start()

    step = gs.shape[0] // grid_sem.shape[0]
    count = gs.shape[0] // step
    grid_loads = [
        pltpu.make_async_copy(grid_h.at[pl.ds(i * step, step)], gs.at[pl.ds(i * step, step)], grid_sem.at[i])
        for i in range(count)
    ]
    start_load(first)
    for copy in grid_loads:
        copy.start()
    for loads in (region_load, far_load, live_load, near_load):
        start_load(loads)

    barrier = pltpu.get_barrier_semaphore()
    for to in greeted:
        pl.semaphore_signal(barrier, inc=1, device_id=(to, d), device_id_type=pl.DeviceIdType.MESH)
    for there, near in sides:
        @pl.when(there)
        def _():
            pl.semaphore_signal(barrier, inc=1, device_id=(g, near), device_id_type=pl.DeviceIdType.MESH)

    for side, (there, _) in enumerate(sides):
        @pl.when(jnp.logical_not(there))
        def _():
            for buf in (nrecv, mnrecv, dnrecv):
                for c in range(CHUNKS):
                    buf[side, c] = jnp.zeros((rows, width), BF16)

    def remote(src, dst, send, recv, to):
        return pltpu.make_async_remote_copy(
            src_ref=src, dst_ref=dst, send_sem=send, recv_sem=recv, device_id=to, device_id_type=pl.DeviceIdType.MESH
        )

    def whole(ref, send, recv):
        return remote(ref, ref, send, recv, (peers[0][0], d))

    def first_axis(h):
        return h % 2

    def far_copy(c, h, kind):
        if not relay:
            return remote(fsend.at[c, kind, h], frecv.at[c, kind, h], fs_sem.at[0], fr_sem.at[c], (peers[kind][0], d))
        to = first_axis(h) if kind < 2 else 1 - first_axis(h)
        if kind == 0:
            return remote(fsend.at[c, 0, h], frelay.at[c, h], fs_sem.at[0], fl_sem.at[c, h], (peers[to][0], d))
        return remote(fsend.at[c, kind, h], frecv.at[c, kind - 1, h], fs_sem.at[0], fr_sem.at[c], (peers[to][0], d))

    def near_copy(c, s):
        return remote(nsend.at[s, c], nrecv.at[1 - s, c], ns_sem.at[s], nr_sem.at[1 - s], (g, sides[s][1]))

    def mfar_copy(c, h, i):
        at = pl.ds(h * piece_rows, piece_rows)
        source, to, recv = msend.at[c, at], i, mfr_sem.at[c, 0]
        if relay:
            if i == 2:
                source, to, recv = mfrecv.at[c, first_axis(h), at], 1 - first_axis(h), mfr_sem.at[c, 1]
            elif i == first_axis(h):
                recv = mfl_sem.at[c, h]
        return remote(source, mfrecv.at[c, i, at], mfs_sem.at[0], recv, (peers[to][0], d))

    def mnear_copy(c, s):
        return remote(msend.at[c], mnrecv.at[1 - s, c], mns_sem.at[s], mnr_sem.at[1 - s], (g, sides[s][1]))

    def dec_copy(c, s):
        return remote(dsend.at[c], dnrecv.at[1 - s, c], ds_sem.at[s], dr_sem.at[1 - s, c], (g, sides[s][1]))

    def start_side(copy, c):
        for s, (there, _) in enumerate(sides):
            @pl.when(there)
            def _():
                copy(c, s).start()

    def wait_side(buf, sem, s):
        @pl.when(sides[s][0])
        def _():
            whole(buf.at[s], sem.at[s], sem.at[s]).wait_recv()

    with scope("ldwait"):
        first[1].wait()
    for c in range(CHUNKS):
        cols = pl.ds(c * width, width)
        for i in range(count):
            if c == 0:
                with scope("gridwait"):
                    grid_loads[i].wait()
            at = pl.ds(i * step, step)
            em[c, at, :] = silu(mm(gs[at, :], wt[0, :, cols])).astype(BF16)
        if c == 0:
            for loads in late:
                start_load(loads)
            with scope("efwait"):
                region_load[1].wait()
                far_load[1].wait()
        far_all = mm(inc[pl.ds(0, long_count)].reshape(long_count * rows, gs.shape[0]), em[c])
        far = [far_all[i * rows:(i + 1) * rows] for i in range(long_count)]

        def toward(i):
            total = None
            for index in range(long_count):
                flag = jnp.where(regions[0, 0, index] == peers[i][0], 1.0, 0.0).astype(F32)
                term = far[index] * flag
                total = term if total is None else total + term
            return total

        if c == 0:
            with scope("barrier"):
                pl.semaphore_wait(barrier, len(greeted) + jnp.where(not_first, 1, 0) + jnp.where(not_last, 1, 0))
        if relay:
            totals = [toward(i) for i in range(far_count)]
            for kind in range(2):
                for h in range(halves):
                    at = slice(h * piece_rows, (h + 1) * piece_rows)
                    axis = first_axis(h)
                    fsend[c, kind, h] = totals[2 if kind == 0 else axis][at].astype(BF16)
                    far_copy(c, h, kind).start()
                    if kind == 0:
                        fheld[c, h] = totals[1 - axis][at]
        else:
            for i in order:
                fsend[c, i, 0] = toward(i).astype(BF16)
                far_copy(c, 0, i).start()

    with scope("enwait"):
        live_load[1].wait()
        near_load[1].wait()
    for k in range(3):
        for t in range(tiles):
            flag = live[0, k, t].astype(F32).astype(BF16)
            at = pl.ds(t * rows, rows)
            inc[long_count + k, :, at] = inc[long_count + k, :, at] * flag
    for c in range(CHUNKS):
        cols = pl.ds(c * width, width)
        near_all = mm(inc[pl.ds(long_count, 3)].reshape(3 * rows, gs.shape[0]), em[c])
        for s, k in ((0, 0), (1, 2)):
            nsend[s, c] = near_all[k * rows:(k + 1) * rows].astype(BF16)
        start_side(near_copy, c)
        own_near[:, cols] = near_all[rows:2 * rows].astype(BF16)

    if relay:
        for c in range(CHUNKS):
            for h in range(halves):
                with scope("relaywait"):
                    far_copy(c, h, 0).wait_recv()
                fsend[c, 2, h] = (fheld[c, h] + frelay[c, h].astype(F32)).astype(BF16)
                far_copy(c, h, 2).start()

    for loads in late:
        loads[1].wait()
    for i in range(far_count):
        total = None
        for index in range(long_count):
            flag = jnp.where(regions[1, 0, index] == peers[i][1], 1.0, 0.0).astype(F32)
            term = pinc[3 + index].astype(F32) * flag
            total = term if total is None else total + term
        proc_inc[i] = total.astype(BF16)
    for k in range(3):
        for t in range(tiles):
            at = pl.ds(t * rows, rows)
            dn[k, at, :] = dn[k, at, :] * live[1, k, t].astype(F32).astype(BF16)

    def node_update(residual, summed, first, second):
        hidden = silu(mm(layer_norm(summed).astype(BF16), wt[first])).astype(BF16)
        return (residual.astype(F32) + mm(hidden, wt[second])).astype(BF16)

    with scope("nearwait"):
        for s in range(2):
            wait_side(nrecv, nr_sem, s)
    parts = []
    for c in range(CHUNKS):
        total = own_near[:, pl.ds(c * width, width)].astype(F32)
        for s in range(2):
            total = total + nrecv[s, c].astype(F32)
        with scope("farwait"):
            whole(frecv.at[c], fr_sem.at[c], fr_sem.at[c]).wait_recv()
        pieces = []
        for h in range(halves):
            piece = total[h * piece_rows:(h + 1) * piece_rows]
            for i in range(frecv.shape[1]):
                piece = piece + frecv[c, i, h].astype(F32)
            pieces.append(piece)
        parts.append(jnp.concatenate(pieces, axis=0))
    with scope("upd1"):
        mesh_mid = node_update(ms[...], jnp.concatenate(parts, axis=1), 1, 2)

    for c in range(CHUNKS):
        msend[c] = silu(mm(mesh_mid, wt[3, :, pl.ds(c * width, width)])).astype(BF16)
        if not relay:
            for i in order:
                mfar_copy(c, 0, i).start()
        else:
            for h in range(halves):
                mfar_copy(c, h, first_axis(h)).start()
        start_side(mnear_copy, c)
    if relay:
        for c in range(CHUNKS):
            for h in range(halves):
                mfar_copy(c, h, 1 - first_axis(h)).start()
    parts = [mm(pinc[1], msend[c]) for c in range(CHUNKS)]
    if relay:
        for c in range(CHUNKS):
            for h in range(halves):
                with scope("mrelaywait"):
                    mfar_copy(c, h, first_axis(h)).wait_recv()
                mfar_copy(c, h, 2).start()
    for s in range(2):
        with scope("mnearwait"):
            wait_side(mnrecv, mnr_sem, s)
        for c in range(CHUNKS):
            parts[c] = parts[c] + mm(pinc[2 * s], mnrecv[s, c])
    for c in range(CHUNKS):
        with scope("mfarwait"):
            if relay:
                whole(mfrecv.at[c, 0], mfr_sem.at[c, 0], mfr_sem.at[c, 0]).wait_recv()
            else:
                whole(mfrecv.at[c], mfr_sem.at[c, 0], mfr_sem.at[c, 0]).wait_recv()
        for i in range(2 if relay else far_count):
            parts[c] = parts[c] + mm(proc_inc[i], mfrecv[c, i])
    if relay:
        for c in range(CHUNKS):
            with scope("mdiagwait"):
                whole(mfrecv.at[c, 2], mfr_sem.at[c, 1], mfr_sem.at[c, 1]).wait_recv()
            parts[c] = parts[c] + mm(proc_inc[2], mfrecv[c, 2])
    with scope("upd2"):
        mesh_next = node_update(mesh_mid, jnp.concatenate(parts, axis=1), 4, 5)
    mesh_out[...] = mesh_next

    for c in range(CHUNKS):
        dsend[c] = silu(mm(mesh_next, wt[6, :, pl.ds(c * width, width)])).astype(BF16)
        start_side(dec_copy, c)

    block = 2 * rows

    def decode(add, c, k, source):
        for i in range(gs.shape[0] // block):
            at = pl.ds(i * block, block)
            part = mm(dn[k, at, :], source)
            acc[at, pl.ds(c * width, width)] = acc[at, pl.ds(c * width, width)] + part if add else part

    with scope("ownpart"):
        for c in range(CHUNKS):
            decode(False, c, 1, dsend[c])
    for s in (near_side, 1 - near_side):
        there = jnp.where(s == 0, not_first, not_last)
        for c in range(CHUNKS):
            with scope("decwait"):
                @pl.when(there)
                def _():
                    whole(dnrecv.at[s, c], dr_sem.at[s, c], dr_sem.at[s, c]).wait_recv()
            decode(True, c, 2 * s, dnrecv[s, c])

    with scope("drain"):
        whole(fsend, fs_sem.at[0], fs_sem.at[0]).wait_send()
        whole(mfrecv, mfs_sem.at[0], mfs_sem.at[0]).wait_send()
        for s, (there, _) in enumerate(sides):
            @pl.when(there)
            def _():
                whole(nsend.at[s], ns_sem.at[s], ns_sem.at[s]).wait_send()
                whole(msend, mns_sem.at[s], mns_sem.at[s]).wait_send()
                whole(dsend, ds_sem.at[s], ds_sem.at[s]).wait_send()


def finish(mesh_v, gs, dw, acc, grid_o, mesh_o, grid_out, out_sem):
    step = gs.shape[0] // (out_sem.shape[0] - 1)
    mesh_copy = pltpu.make_async_copy(mesh_v, mesh_o, out_sem.at[0])
    mesh_copy.start()
    outs = []
    for i in range(gs.shape[0] // step):
        at = pl.ds(i * step, step)
        hidden = silu(mm(layer_norm(acc[at, :]).astype(BF16), dw[0])).astype(BF16)
        grid_out[at, :] = (gs[at, :].astype(F32) + mm(hidden, dw[1])).astype(BF16)
        copy = pltpu.make_async_copy(grid_out.at[at], grid_o.at[at], out_sem.at[1 + i])
        copy.start()
        outs.append(copy)
    with scope("outwait"):
        mesh_copy.wait()
        for copy in outs:
            copy.wait()


def body(groups, devs, *args):
    grid_state, mesh_state = args[0], args[1]
    args = list(args)
    args[14], args[17] = args[14].T, args[17].T
    encode_live, encode_far, encode_groups, decode_near = args[12], args[13], args[14], args[18]
    grid_rows, feats = grid_state.shape
    rows = mesh_state.shape[0]
    width = feats // CHUNKS
    far_count = groups - 1
    long_count = encode_far.shape[0]

    def vmem(*shape, dtype=BF16):
        return pltpu.VMEM(shape, dtype)

    dma = pltpu.SemaphoreType.DMA
    relay = groups == 4
    halves = 2 if relay else 1
    piece = (rows // halves, width)
    block = (rows, width)
    scratch = [
        vmem(rows, feats), vmem(7, feats, feats), vmem(3 + long_count, rows, grid_rows),
        pltpu.SMEM((2, *encode_live.shape), jnp.int32), pltpu.SMEM((2, *encode_groups.shape), jnp.int32),
        vmem(3 + long_count, rows, rows), vmem(*decode_near.shape),
        vmem(CHUNKS, grid_rows, width),
        vmem(CHUNKS, halves, *piece, dtype=F32), vmem(CHUNKS, far_count, halves, *piece),
        vmem(CHUNKS, halves, *piece), vmem(CHUNKS, 2 if relay else far_count, halves, *piece),
        vmem(2, CHUNKS, *block), vmem(2, CHUNKS, *block),
        vmem(CHUNKS, *block), vmem(CHUNKS, far_count, *block), vmem(2, CHUNKS, *block),
        vmem(CHUNKS, *block), vmem(2, CHUNKS, *block),
        vmem(rows, feats), vmem(far_count, rows, rows),
        dma((11,)), dma((GRID_LOADS,)), dma((1,)), dma((CHUNKS, halves)), dma((CHUNKS,)), dma((2,)), dma((2,)),
        dma((1,)), dma((CHUNKS, halves)), dma((CHUNKS, halves)), dma((2,)), dma((2,)), dma((2,)), dma((2, CHUNKS)),
    ]
    hbm = pl.BlockSpec(memory_space=pltpu.HBM)
    on_chip = pl.BlockSpec(memory_space=pltpu.VMEM)
    held = pl.pallas_call(
        functools.partial(exchange, groups, devs),
        out_shape=(
            vmem(*mesh_state.shape), vmem(*grid_state.shape), vmem(2, feats, feats), vmem(*grid_state.shape, dtype=F32),
        ),
        in_specs=[hbm] * len(args),
        out_specs=(on_chip,) * 4,
        scratch_shapes=scratch,
        compiler_params=pltpu.CompilerParams(collective_id=0, has_side_effects=True, vmem_limit_bytes=32 << 20),
        name="exchange",
    )(*(pltpu.with_memory_space_constraint(arg, pltpu.HBM) for arg in args))
    return pl.pallas_call(
        finish,
        out_shape=(
            jax.ShapeDtypeStruct(grid_state.shape, BF16),
            jax.ShapeDtypeStruct(mesh_state.shape, BF16),
        ),
        in_specs=[on_chip] * 4,
        out_specs=(hbm, hbm),
        scratch_shapes=[vmem(*grid_state.shape), dma((1 + GRID_OUTS,))],
        compiler_params=pltpu.CompilerParams(vmem_limit_bytes=16 << 20),
        name="finish",
    )(*held)


def solution(mesh):
    both = ("group", "dev")
    row, whole, second = P(both, None), P(), P(None, both, None)
    flags = P(None, both)
    return jax.shard_map(
        functools.partial(body, mesh.shape["group"], mesh.shape["dev"]),
        mesh=mesh,
        in_specs=(
            row, row, whole, whole, whole, whole, whole, whole, whole, whole, whole,
            second, flags, second, flags, second, second, flags, second, flags,
        ),
        out_specs=(row, row),
        check_vma=False,
    )
```

time: 33.7 us -> 28.9 us (0.86)
  local copies, waits for them, and re-layouts: 2.96 us -> 0 us
  Pallas kernels: 29.9 us -> 28.1 us
    unnamed x4 -> x0, local copies, waits for them, and re-layouts: 2.96 us -> none
    pallas_call x1 -> x2, Pallas kernels: 29.9 us -> 28.1 us  [the longest x1 25.4 us: body(): pl.pallas_call(functools.partial(exchange, groups, devs), out_shape=(vmem...]
where the time goes in v1:
time: 28.9 us; the launch traced here: 28.7 us
  Pallas kernels  28.1 us (97%)
  between operations  0.65 us (2%)
    pallas_call x1, Pallas kernels, body(): pl.pallas_call(functools.partial(exchange, groups, devs), out_shape=(vmem...  25.4 us
    pallas_call x1, Pallas kernels, body(): pl.pallas_call(finish, out_shape=(jax.ShapeDtypeStruct(grid_state.shape,...  2.66 us

profile of v1, /device:TPU:1, one launch (start us, length us, event | category | flops | bytes accessed | tf_op | source)
XLA Modules:
  0.0 28.7 jit_solution(16358784415614948242)
XLA Ops:
  0.6 25.4 %exchange.1 = (bf16[128,512]{1,0:T(8,128)(2,1)S(1)}, bf16[1024,512]{1,0:T(8,128)(2,1)S(1)}, bf16[2,512,512]{2,1,0:T(8,128)(2,1)S(1)}, f32[1024,512]{1,0:T(8,128)S(1)}) custom-call(bf16[1024,512]{1,0:T(8,128)(2,1)} %grid_h.1, bf16[128,512]{1,0:T(8,128)(2,1)} %mesh_h.1, bf16[512,512]{1,0:T(8,128)(2,1)} %ee_h.1, bf16[512,512]{1,0:T(8,128)(2,1)} %e1_h.1, ...), custom_call_target="tpu_custom_call" | custom-call | tf_op jit(solution)/shard_map/exchange/pallas_call | solution.py:418
  26.1 2.7 %finish.1 = (bf16[1024,512]{1,0:T(8,128)(2,1)}, bf16[128,512]{1,0:T(8,128)(2,1)}) custom-call(bf16[128,512]{1,0:T(8,128)(2,1)S(1)} %get-tuple-element.6.mesh_v, bf16[1024,512]{1,0:T(8,128)(2,1)S(1)} %get-tuple-element.7.gs, bf16[2,512,512]{2,1,0:T(8,128)(2,1)S(1)} %get-tuple-element.8.dw, f32[1024,512]{1,0:T(8,128)S(1)} %get-tuple-element.9.acc), custom_call_target="tpu_custom_call" | custom-call | tf_op jit(solution)/shard_map/finish/pallas_call | solution.py:429

commit v2 on v1

--- a/solution.py
+++ b/solution.py
@@ -12,7 +12,11 @@
 F32 = jnp.float32
 CHUNKS = 2
 GRID_LOADS = 2
-GRID_OUTS = 4
+GRID_OUTS = 2
+DIRECT_RS = True
+DIRECT_AG = True
+DEFER_RS = True
+DEFER_AG = False
 
 
 def silu(x):
@@ -69,15 +73,14 @@
     relay = groups == 4
     halves = fsend.shape[2]
     piece_rows = rows // halves
-    if relay:
-        greeted = [to for to, _ in peers[:2]]
-    elif groups & (groups - 1):
+    if groups & (groups - 1):
         greeted = [to for to, _ in peers] + [source for _, source in peers]
     else:
         greeted = [to for to, _ in peers]
     not_first, not_last = d > 0, d < devs - 1
     sides = ((not_first, d - 1), (not_last, d + 1))
     near_side = 1 - lax.rem(d, 2)
+    even, odd = lax.rem(d, 2) == 0, lax.rem(d, 2) == 1
 
     def load(index, pairs, whole):
         starts = [pltpu.make_async_copy(src, dst, load_sem.at[index]) for src, dst in pairs]
@@ -129,6 +132,17 @@
                 for c in range(CHUNKS):
                     buf[side, c] = jnp.zeros((rows, width), BF16)
 
+    def direct_rs(c):
+        return relay and DIRECT_RS and c == CHUNKS - 1
+
+    def direct_ag(c):
+        return relay and DIRECT_AG and c == CHUNKS - 1
+
+    if relay:
+        @pl.when(odd)
+        def _():
+            frecv[CHUNKS - 1, 2] = jnp.zeros(frecv.shape[2:], BF16)
+
     def remote(src, dst, send, recv, to):
         return pltpu.make_async_remote_copy(
             src_ref=src, dst_ref=dst, send_sem=send, recv_sem=recv, device_id=to, device_id_type=pl.DeviceIdType.MESH
@@ -147,6 +161,12 @@
         if kind == 0:
             return remote(fsend.at[c, 0, h], frelay.at[c, h], fs_sem.at[0], fl_sem.at[c, h], (peers[to][0], d))
         return remote(fsend.at[c, kind, h], frecv.at[c, kind - 1, h], fs_sem.at[0], fr_sem.at[c], (peers[to][0], d))
+
+    def far_direct(c):
+        return remote(fsend.at[c, 0], frecv.at[c, 2], fs_sem.at[0], fr_sem.at[c], (peers[2][0], d))
+
+    def mfar_direct(c):
+        return remote(msend.at[c], mfrecv.at[c, 2], mfs_sem.at[0], mfr_sem.at[c, 1], (peers[2][0], d))
 
     def near_copy(c, s):
         return remote(nsend.at[s, c], nrecv.at[1 - s, c], ns_sem.at[s], nr_sem.at[1 - s], (g, sides[s][1]))
@@ -178,6 +198,7 @@
         def _():
             whole(buf.at[s], sem.at[s], sem.at[s]).wait_recv()
 
+    greetings = len(greeted) + jnp.where(not_first, 1, 0) + jnp.where(not_last, 1, 0)
     with scope("ldwait"):
         first[1].wait()
     for c in range(CHUNKS):
@@ -186,14 +207,12 @@
             if c == 0:
                 with scope("gridwait"):
                     grid_loads[i].wait()
+                    if i == count - 1:
+                        region_load[1].wait()
+                        far_load[1].wait()
+                        pl.semaphore_wait(barrier, greetings)
             at = pl.ds(i * step, step)
             em[c, at, :] = silu(mm(gs[at, :], wt[0, :, cols])).astype(BF16)
-        if c == 0:
-            for loads in late:
-                start_load(loads)
-            with scope("efwait"):
-                region_load[1].wait()
-                far_load[1].wait()
         far_all = mm(inc[pl.ds(0, long_count)].reshape(long_count * rows, gs.shape[0]), em[c])
         far = [far_all[i * rows:(i + 1) * rows] for i in range(long_count)]
 
@@ -205,9 +224,6 @@
                 total = term if total is None else total + term
             return total
 
-        if c == 0:
-            with scope("barrier"):
-                pl.semaphore_wait(barrier, len(greeted) + jnp.where(not_first, 1, 0) + jnp.where(not_last, 1, 0))
         if relay:
             totals = [toward(i) for i in range(far_count)]
             for kind in range(2):
@@ -215,14 +231,37 @@
                     at = slice(h * piece_rows, (h + 1) * piece_rows)
                     axis = first_axis(h)
                     fsend[c, kind, h] = totals[2 if kind == 0 else axis][at].astype(BF16)
-                    far_copy(c, h, kind).start()
                     if kind == 0:
                         fheld[c, h] = totals[1 - axis][at]
+                        if direct_rs(c):
+                            fsend[c, 2, h] = totals[1 - axis][at].astype(BF16)
+
+            @pl.when(even)
+            def _():
+                if direct_rs(c):
+                    far_direct(c).start()
+                for kind in range(1 if direct_rs(c) else 0, 3 if direct_rs(c) else 2):
+                    for h in range(halves):
+                        far_copy(c, h, kind).start()
+
+            @pl.when(odd)
+            def _():
+                for h in range(halves):
+                    far_copy(c, h, 0).start()
+                if not DEFER_RS:
+                    for h in range(halves):
+                        far_copy(c, h, 1).start()
+                elif c == CHUNKS - 1:
+                    for b in range(CHUNKS):
+                        for h in range(halves):
+                            far_copy(b, h, 1).start()
         else:
             for i in order:
                 fsend[c, i, 0] = toward(i).astype(BF16)
                 far_copy(c, 0, i).start()
 
+    for loads in late:
+        start_load(loads)
     with scope("enwait"):
         live_load[1].wait()
         near_load[1].wait()
@@ -240,12 +279,20 @@
         own_near[:, cols] = near_all[rows:2 * rows].astype(BF16)
 
     if relay:
-        for c in range(CHUNKS):
+        def pass_on(c):
             for h in range(halves):
                 with scope("relaywait"):
                     far_copy(c, h, 0).wait_recv()
                 fsend[c, 2, h] = (fheld[c, h] + frelay[c, h].astype(F32)).astype(BF16)
                 far_copy(c, h, 2).start()
+
+        for c in range(CHUNKS):
+            if direct_rs(c):
+                @pl.when(odd)
+                def _():
+                    pass_on(c)
+            else:
+                pass_on(c)
 
     for loads in late:
         loads[1].wait()
@@ -273,12 +320,22 @@
         total = own_near[:, pl.ds(c * width, width)].astype(F32)
         for s in range(2):
             total = total + nrecv[s, c].astype(F32)
+        slots = 3 if direct_rs(c) else 2 if relay else far_count
         with scope("farwait"):
-            whole(frecv.at[c], fr_sem.at[c], fr_sem.at[c]).wait_recv()
+            if direct_rs(c):
+                @pl.when(even)
+                def _():
+                    whole(frecv.at[c], fr_sem.at[c], fr_sem.at[c]).wait_recv()
+
+                @pl.when(odd)
+                def _():
+                    whole(frecv.at[c, pl.ds(0, 2)], fr_sem.at[c], fr_sem.at[c]).wait_recv()
+            else:
+                whole(frecv.at[c, pl.ds(0, slots)], fr_sem.at[c], fr_sem.at[c]).wait_recv()
         pieces = []
         for h in range(halves):
             piece = total[h * piece_rows:(h + 1) * piece_rows]
-            for i in range(frecv.shape[1]):
+            for i in range(slots):
                 piece = piece + frecv[c, i, h].astype(F32)
             pieces.append(piece)
         parts.append(jnp.concatenate(pieces, axis=0))
@@ -293,18 +350,35 @@
         else:
             for h in range(halves):
                 mfar_copy(c, h, first_axis(h)).start()
+            if direct_ag(c):
+                @pl.when(even)
+                def _():
+                    mfar_direct(c).start()
         start_side(mnear_copy, c)
-    if relay:
+
+    def send_second():
         for c in range(CHUNKS):
             for h in range(halves):
                 mfar_copy(c, h, 1 - first_axis(h)).start()
+
+    if relay and DEFER_AG:
+        pl.when(even)(send_second)
+    elif relay:
+        send_second()
     parts = [mm(pinc[1], msend[c]) for c in range(CHUNKS)]
     if relay:
         for c in range(CHUNKS):
             for h in range(halves):
                 with scope("mrelaywait"):
                     mfar_copy(c, h, first_axis(h)).wait_recv()
-                mfar_copy(c, h, 2).start()
+                if direct_ag(c):
+                    @pl.when(odd)
+                    def _():
+                        mfar_copy(c, h, 2).start()
+                else:
+                    mfar_copy(c, h, 2).start()
+        if DEFER_AG:
+            pl.when(odd)(send_second)
     for s in range(2):
         with scope("mnearwait"):
             wait_side(mnrecv, mnr_sem, s)
@@ -364,13 +438,18 @@
 
 def finish(mesh_v, gs, dw, acc, grid_o, mesh_o, grid_out, out_sem):
     step = gs.shape[0] // (out_sem.shape[0] - 1)
+    width = gs.shape[1] // CHUNKS
     mesh_copy = pltpu.make_async_copy(mesh_v, mesh_o, out_sem.at[0])
     mesh_copy.start()
     outs = []
     for i in range(gs.shape[0] // step):
         at = pl.ds(i * step, step)
-        hidden = silu(mm(layer_norm(acc[at, :]).astype(BF16), dw[0])).astype(BF16)
-        grid_out[at, :] = (gs[at, :].astype(F32) + mm(hidden, dw[1])).astype(BF16)
+        normed = layer_norm(acc[at, :]).astype(BF16)
+        parts = [silu(mm(normed, dw[0, :, pl.ds(c * width, width)])).astype(BF16) for c in range(CHUNKS)]
+        hidden = jnp.concatenate(parts, axis=1)
+        for c in range(CHUNKS):
+            cols = pl.ds(c * width, width)
+            grid_out[at, cols] = (gs[at, cols].astype(F32) + mm(hidden, dw[1, :, cols])).astype(BF16)
         copy = pltpu.make_async_copy(grid_out.at[at], grid_o.at[at], out_sem.at[1 + i])
         copy.start()
         outs.append(copy)
@@ -405,7 +484,7 @@
         vmem(3 + long_count, rows, rows), vmem(*decode_near.shape),
         vmem(CHUNKS, grid_rows, width),
         vmem(CHUNKS, halves, *piece, dtype=F32), vmem(CHUNKS, far_count, halves, *piece),
-        vmem(CHUNKS, halves, *piece), vmem(CHUNKS, 2 if relay else far_count, halves, *piece),
+        vmem(CHUNKS, halves, *piece), vmem(CHUNKS, far_count, halves, *piece),
         vmem(2, CHUNKS, *block), vmem(2, CHUNKS, *block),
         vmem(CHUNKS, *block), vmem(CHUNKS, far_count, *block), vmem(2, CHUNKS, *block),
         vmem(CHUNKS, *block), vmem(2, CHUNKS, *block),

time: 28.9 us -> 27.7 us (0.958)
  Pallas kernels: 28.1 us -> 26.9 us
    pallas_call x1, Pallas kernels: 25.4 us -> 24.4 us  [body(): pl.pallas_call(functools.partial(exchange, groups, devs), out_shape=(vmem...]
where the time goes in v2:
time: 27.7 us; the launch traced here: 27.6 us
  Pallas kernels  26.9 us (97%)
  between operations  0.65 us (2%)
    pallas_call x1, Pallas kernels, body(): pl.pallas_call(functools.partial(exchange, groups, devs), out_shape=(vmem...  24.4 us
    pallas_call x1, Pallas kernels, body(): pl.pallas_call(finish, out_shape=(jax.ShapeDtypeStruct(grid_state.shape,...  2.55 us

profile of v2, /device:TPU:1, one launch (start us, length us, event | category | flops | bytes accessed | tf_op | source)
XLA Modules:
  0.0 27.6 jit_solution(3154749107732505801)
XLA Ops:
  0.6 24.4 %exchange.1 = (bf16[128,512]{1,0:T(8,128)(2,1)S(1)}, bf16[1024,512]{1,0:T(8,128)(2,1)S(1)}, bf16[2,512,512]{2,1,0:T(8,128)(2,1)S(1)}, f32[1024,512]{1,0:T(8,128)S(1)}) custom-call(bf16[1024,512]{1,0:T(8,128)(2,1)} %grid_h.1, bf16[128,512]{1,0:T(8,128)(2,1)} %mesh_h.1, bf16[512,512]{1,0:T(8,128)(2,1)} %ee_h.1, bf16[512,512]{1,0:T(8,128)(2,1)} %e1_h.1, ...), custom_call_target="tpu_custom_call" | custom-call | tf_op jit(solution)/shard_map/exchange/pallas_call | solution.py:497
  25.0 2.6 %finish.1 = (bf16[1024,512]{1,0:T(8,128)(2,1)}, bf16[128,512]{1,0:T(8,128)(2,1)}) custom-call(bf16[128,512]{1,0:T(8,128)(2,1)S(1)} %get-tuple-element.6.mesh_v, bf16[1024,512]{1,0:T(8,128)(2,1)S(1)} %get-tuple-element.7.gs, bf16[2,512,512]{2,1,0:T(8,128)(2,1)S(1)} %get-tuple-element.8.dw, f32[1024,512]{1,0:T(8,128)S(1)} %get-tuple-element.9.acc), custom_call_target="tpu_custom_call" | custom-call | tf_op jit(solution)/shard_map/finish/pallas_call | solution.py:508

commit v3 on v2

--- a/solution.py
+++ b/solution.py
@@ -13,10 +13,8 @@
 CHUNKS = 2
 GRID_LOADS = 2
 GRID_OUTS = 2
-DIRECT_RS = True
-DIRECT_AG = True
-DEFER_RS = True
-DEFER_AG = False
+DIRECT_RS = 0
+DIRECT_AG = 0
 
 
 def silu(x):
@@ -59,7 +57,7 @@
     ms, wt, inc, live, regions, pinc, dn,
     em, fheld, fsend, frelay, frecv, nsend, nrecv, msend, mfrecv, mnrecv, dsend, dnrecv,
     own_near, proc_inc,
-    load_sem, grid_sem, fs_sem, fl_sem, fr_sem, ns_sem, nr_sem, mfs_sem, mfl_sem, mfr_sem, mns_sem, mnr_sem, ds_sem, dr_sem,
+    load_sem, grid_sem, fs_sem, fl_sem, fr_sem, ns_sem, nr_sem, mfs_sem, mfl_sem, mfr_sem, mns_sem, mnr_sem, ds_sem, dr_sem, turn,
 ):
     g = lax.axis_index("group")
     d = lax.axis_index("dev")
@@ -133,15 +131,16 @@
                     buf[side, c] = jnp.zeros((rows, width), BF16)
 
     def direct_rs(c):
-        return relay and DIRECT_RS and c == CHUNKS - 1
+        return relay and c >= DIRECT_RS
 
     def direct_ag(c):
-        return relay and DIRECT_AG and c == CHUNKS - 1
+        return relay and c >= DIRECT_AG
 
     if relay:
         @pl.when(odd)
         def _():
-            frecv[CHUNKS - 1, 2] = jnp.zeros(frecv.shape[2:], BF16)
+            for c in range(DIRECT_RS, CHUNKS):
+                frecv[c, 2] = jnp.zeros(frecv.shape[2:], BF16)
 
     def remote(src, dst, send, recv, to):
         return pltpu.make_async_remote_copy(
@@ -151,22 +150,27 @@
     def whole(ref, send, recv):
         return remote(ref, ref, send, recv, (peers[0][0], d))
 
+    def hand_over(phase):
+        @pl.when(not_last)
+        def _():
+            pl.semaphore_signal(turn.at[phase], inc=1, device_id=(g, d + 1), device_id_type=pl.DeviceIdType.MESH)
+
     def first_axis(h):
         return h % 2
 
     def far_copy(c, h, kind):
         if not relay:
-            return remote(fsend.at[c, kind, h], frecv.at[c, kind, h], fs_sem.at[0], fr_sem.at[c], (peers[kind][0], d))
+            return remote(fsend.at[c, kind, h], frecv.at[c, kind, h], fs_sem.at[c], fr_sem.at[c], (peers[kind][0], d))
         to = first_axis(h) if kind < 2 else 1 - first_axis(h)
         if kind == 0:
-            return remote(fsend.at[c, 0, h], frelay.at[c, h], fs_sem.at[0], fl_sem.at[c, h], (peers[to][0], d))
-        return remote(fsend.at[c, kind, h], frecv.at[c, kind - 1, h], fs_sem.at[0], fr_sem.at[c], (peers[to][0], d))
+            return remote(fsend.at[c, 0, h], frelay.at[c, h], fs_sem.at[c], fl_sem.at[c, h], (peers[to][0], d))
+        return remote(fsend.at[c, kind, h], frecv.at[c, kind - 1, h], fs_sem.at[c], fr_sem.at[c], (peers[to][0], d))
 
     def far_direct(c):
-        return remote(fsend.at[c, 0], frecv.at[c, 2], fs_sem.at[0], fr_sem.at[c], (peers[2][0], d))
+        return remote(fsend.at[c, 0], frecv.at[c, 2], fs_sem.at[c], fr_sem.at[c], (peers[2][0], d))
 
     def mfar_direct(c):
-        return remote(msend.at[c], mfrecv.at[c, 2], mfs_sem.at[0], mfr_sem.at[c, 1], (peers[2][0], d))
+        return remote(msend.at[c], mfrecv.at[c, 2], mfs_sem.at[c], mfr_sem.at[c, 1], (peers[2][0], d))
 
     def near_copy(c, s):
         return remote(nsend.at[s, c], nrecv.at[1 - s, c], ns_sem.at[s], nr_sem.at[1 - s], (g, sides[s][1]))
@@ -179,7 +183,7 @@
                 source, to, recv = mfrecv.at[c, first_axis(h), at], 1 - first_axis(h), mfr_sem.at[c, 1]
             elif i == first_axis(h):
                 recv = mfl_sem.at[c, h]
-        return remote(source, mfrecv.at[c, i, at], mfs_sem.at[0], recv, (peers[to][0], d))
+        return remote(source, mfrecv.at[c, i, at], mfs_sem.at[c], recv, (peers[to][0], d))
 
     def mnear_copy(c, s):
         return remote(msend.at[c], mnrecv.at[1 - s, c], mns_sem.at[s], mnr_sem.at[1 - s], (g, sides[s][1]))
@@ -244,17 +248,6 @@
                     for h in range(halves):
                         far_copy(c, h, kind).start()
 
-            @pl.when(odd)
-            def _():
-                for h in range(halves):
-                    far_copy(c, h, 0).start()
-                if not DEFER_RS:
-                    for h in range(halves):
-                        far_copy(c, h, 1).start()
-                elif c == CHUNKS - 1:
-                    for b in range(CHUNKS):
-                        for h in range(halves):
-                            far_copy(b, h, 1).start()
         else:
             for i in order:
                 fsend[c, i, 0] = toward(i).astype(BF16)
@@ -279,6 +272,21 @@
         own_near[:, cols] = near_all[rows:2 * rows].astype(BF16)
 
     if relay:
+        @pl.when(even)
+        def _():
+            with scope("rsdrain"):
+                whole(fsend.at[0], fs_sem.at[0], fs_sem.at[0]).wait_send()
+            hand_over(0)
+
+        @pl.when(odd)
+        def _():
+            with scope("rsturn"):
+                pl.semaphore_wait(turn.at[0], 1)
+            for kind in range(2):
+                for c in range(CHUNKS):
+                    for h in range(halves):
+                        far_copy(c, h, kind).start()
+
         def pass_on(c):
             for h in range(halves):
                 with scope("relaywait"):
@@ -348,12 +356,13 @@
             for i in order:
                 mfar_copy(c, 0, i).start()
         else:
-            for h in range(halves):
-                mfar_copy(c, h, first_axis(h)).start()
-            if direct_ag(c):
-                @pl.when(even)
-                def _():
+            @pl.when(even)
+            def _():
+                if direct_ag(c):
                     mfar_direct(c).start()
+                for h in range(halves):
+                    mfar_copy(c, h, first_axis(h)).start()
+                    mfar_copy(c, h, 1 - first_axis(h)).start()
         start_side(mnear_copy, c)
 
     def send_second():
@@ -361,11 +370,22 @@
             for h in range(halves):
                 mfar_copy(c, h, 1 - first_axis(h)).start()
 
-    if relay and DEFER_AG:
-        pl.when(even)(send_second)
-    elif relay:
-        send_second()
+    if relay:
+        @pl.when(odd)
+        def _():
+            with scope("oddwait"):
+                pl.semaphore_wait(turn.at[1], 1)
+            for c in range(CHUNKS):
+                for h in range(halves):
+                    mfar_copy(c, h, first_axis(h)).start()
+            send_second()
     parts = [mm(pinc[1], msend[c]) for c in range(CHUNKS)]
+    if relay:
+        @pl.when(even)
+        def _():
+            with scope("agdrain"):
+                whole(mfrecv.at[0], mfs_sem.at[0], mfs_sem.at[0]).wait_send()
+            hand_over(1)
     if relay:
         for c in range(CHUNKS):
             for h in range(halves):
@@ -377,8 +397,6 @@
                         mfar_copy(c, h, 2).start()
                 else:
                     mfar_copy(c, h, 2).start()
-        if DEFER_AG:
-            pl.when(odd)(send_second)
     for s in range(2):
         with scope("mnearwait"):
             wait_side(mnrecv, mnr_sem, s)
@@ -426,8 +444,15 @@
             decode(True, c, 2 * s, dnrecv[s, c])
 
     with scope("drain"):
-        whole(fsend, fs_sem.at[0], fs_sem.at[0]).wait_send()
-        whole(mfrecv, mfs_sem.at[0], mfs_sem.at[0]).wait_send()
+        def far_sent(c):
+            whole(fsend.at[c], fs_sem.at[c], fs_sem.at[c]).wait_send()
+            whole(mfrecv.at[c], mfs_sem.at[c], mfs_sem.at[c]).wait_send()
+
+        for c in range(CHUNKS):
+            if relay and c == 0:
+                pl.when(odd)(functools.partial(far_sent, c))
+            else:
+                far_sent(c)
         for s, (there, _) in enumerate(sides):
             @pl.when(there)
             def _():
@@ -489,8 +514,8 @@
         vmem(CHUNKS, *block), vmem(CHUNKS, far_count, *block), vmem(2, CHUNKS, *block),
         vmem(CHUNKS, *block), vmem(2, CHUNKS, *block),
         vmem(rows, feats), vmem(far_count, rows, rows),
-        dma((11,)), dma((GRID_LOADS,)), dma((1,)), dma((CHUNKS, halves)), dma((CHUNKS,)), dma((2,)), dma((2,)),
-        dma((1,)), dma((CHUNKS, halves)), dma((CHUNKS, halves)), dma((2,)), dma((2,)), dma((2,)), dma((2, CHUNKS)),
+        dma((11,)), dma((GRID_LOADS,)), dma((CHUNKS,)), dma((CHUNKS, halves)), dma((CHUNKS,)), dma((2,)), dma((2,)),
+        dma((CHUNKS,)), dma((CHUNKS, halves)), dma((CHUNKS, halves)), dma((2,)), dma((2,)), dma((2,)), dma((2, CHUNKS)), pltpu.SemaphoreType.REGULAR((2,)),
     ]
     hbm = pl.BlockSpec(memory_space=pltpu.HBM)
     on_chip = pl.BlockSpec(memory_space=pltpu.VMEM)

time: 27.7 us -> 26.5 us (0.957)
  Pallas kernels: 26.9 us -> 25.7 us
    pallas_call x1, Pallas kernels: 24.4 us -> 23.1 us  [body(): pl.pallas_call(functools.partial(exchange, groups, devs), out_shape=(vmem...]
where the time goes in v3:
time: 26.5 us; the launch traced here: 26.3 us
  Pallas kernels  25.7 us (97%)
  between operations  0.65 us (2%)
    pallas_call x1, Pallas kernels, body(): pl.pallas_call(functools.partial(exchange, groups, devs), out_shape=(vmem...  23.1 us
    pallas_call x1, Pallas kernels, body(): pl.pallas_call(finish, out_shape=(jax.ShapeDtypeStruct(grid_state.shape,...  2.54 us

profile of v3, /device:TPU:1, one launch (start us, length us, event | category | flops | bytes accessed | tf_op | source)
XLA Modules:
  0.0 26.3 jit_solution(16841663262378342498)
XLA Ops:
  0.6 23.1 %exchange.1 = (bf16[128,512]{1,0:T(8,128)(2,1)S(1)}, bf16[1024,512]{1,0:T(8,128)(2,1)S(1)}, bf16[2,512,512]{2,1,0:T(8,128)(2,1)S(1)}, f32[1024,512]{1,0:T(8,128)S(1)}) custom-call(bf16[1024,512]{1,0:T(8,128)(2,1)} %grid_h.1, bf16[128,512]{1,0:T(8,128)(2,1)} %mesh_h.1, bf16[512,512]{1,0:T(8,128)(2,1)} %ee_h.1, bf16[512,512]{1,0:T(8,128)(2,1)} %e1_h.1, ...), custom_call_target="tpu_custom_call" | custom-call | tf_op jit(solution)/shard_map/exchange/pallas_call | solution.py:522
  23.8 2.5 %finish.1 = (bf16[1024,512]{1,0:T(8,128)(2,1)}, bf16[128,512]{1,0:T(8,128)(2,1)}) custom-call(bf16[128,512]{1,0:T(8,128)(2,1)S(1)} %get-tuple-element.6.mesh_v, bf16[1024,512]{1,0:T(8,128)(2,1)S(1)} %get-tuple-element.7.gs, bf16[2,512,512]{2,1,0:T(8,128)(2,1)S(1)} %get-tuple-element.8.dw, f32[1024,512]{1,0:T(8,128)S(1)} %get-tuple-element.9.acc), custom_call_target="tpu_custom_call" | custom-call | tf_op jit(solution)/shard_map/finish/pallas_call | solution.py:533

commit v4 on v3

--- a/solution.py
+++ b/solution.py
@@ -11,26 +11,28 @@
 BF16 = jnp.bfloat16
 F32 = jnp.float32
 CHUNKS = 2
-GRID_LOADS = 2
+GRID_CUT = 4
 GRID_OUTS = 2
-DIRECT_RS = 0
-DIRECT_AG = 0
+ODD_RS = 1
+ODD_AG = 1
+
+
+def gate(half):
+    return half + half * jnp.tanh(half)
 
 
 def silu(x):
-    half = 0.5 * x
-    return half + half * jnp.tanh(half)
+    return gate(0.5 * x)
 
 
 def mm(a, b):
     return jnp.dot(a, b, preferred_element_type=F32)
 
 
-def layer_norm(v):
-    mean = jnp.mean(v, axis=-1, keepdims=True)
-    cent = v - mean
+def centred(v):
+    cent = v - jnp.mean(v, axis=-1, keepdims=True)
     var = jnp.mean(cent * cent, axis=-1, keepdims=True)
-    return cent * lax.rsqrt(var + 1e-05)
+    return cent.astype(BF16), 0.5 * lax.rsqrt(var + 1e-05)
 
 
 def partner(me, r, count):
@@ -53,8 +55,8 @@
     devs,
     grid_h, mesh_h, ee_h, e1_h, e2_h, pe_h, p1_h, p2_h, de_h, d1_h, d2_h,
     en_h, el_h, ef_h, eg_h, pn_h, pf_h, pg_h, dn_h, dl_h,
-    mesh_out, gs, dw, acc,
-    ms, wt, inc, live, regions, pinc, dn,
+    mesh_out, gs, dw, acc, dn, last,
+    ms, wt, inc, live, regions, pinc,
     em, fheld, fsend, frelay, frecv, nsend, nrecv, msend, mfrecv, mnrecv, dsend, dnrecv,
     own_near, proc_inc,
     load_sem, grid_sem, fs_sem, fl_sem, fr_sem, ns_sem, nr_sem, mfs_sem, mfl_sem, mfr_sem, mns_sem, mnr_sem, ds_sem, dr_sem, turn,
@@ -77,7 +79,8 @@
         greeted = [to for to, _ in peers]
     not_first, not_last = d > 0, d < devs - 1
     sides = ((not_first, d - 1), (not_last, d + 1))
-    near_side = 1 - lax.rem(d, 2)
+    far_side = lax.rem(d, 2)
+    near_side = 1 - far_side
     even, odd = lax.rem(d, 2) == 0, lax.rem(d, 2) == 1
 
     def load(index, pairs, whole):
@@ -92,23 +95,20 @@
     region_load = load(4, [(eg_h, regions.at[0]), (pg_h, regions.at[1])], regions)
     late = [
         load(5, [(mesh_h, ms)], ms),
-        load(6, [(e1_h, wt.at[1]), (e2_h, wt.at[2]), (pe_h, wt.at[3])], wt.at[pl.ds(1, 3)]),
+        load(6, [(h, wt.at[1 + i]) for i, h in enumerate((e1_h, e2_h, pe_h, p1_h, p2_h, de_h))], wt.at[pl.ds(1, 6)]),
         load(7, [(pn_h, pinc.at[pl.ds(0, 3)]), (pf_h, pinc.at[pl.ds(3, long_count)])], pinc),
         load(8, [(dn_h, dn)], dn),
-        load(9, [(p1_h, wt.at[4]), (p2_h, wt.at[5]), (de_h, wt.at[6])], wt.at[pl.ds(4, 3)]),
-        load(10, [(d1_h, dw.at[0]), (d2_h, dw.at[1])], dw),
+        load(9, [(d1_h, dw.at[0]), (d2_h, dw.at[1])], dw),
     ]
 
     def start_load(loads):
         for copy in loads[0]:
             copy.start()
 
-    step = gs.shape[0] // grid_sem.shape[0]
-    count = gs.shape[0] // step
-    grid_loads = [
-        pltpu.make_async_copy(grid_h.at[pl.ds(i * step, step)], gs.at[pl.ds(i * step, step)], grid_sem.at[i])
-        for i in range(count)
-    ]
+    cut = gs.shape[0] // GRID_CUT
+    grid_rows = [pl.ds(0, cut), pl.ds(cut, gs.shape[0] - cut)]
+    count = len(grid_rows)
+    grid_loads = [pltpu.make_async_copy(grid_h.at[at], gs.at[at], grid_sem.at[i]) for i, at in enumerate(grid_rows)]
     start_load(first)
     for copy in grid_loads:
         copy.start()
@@ -130,16 +130,10 @@
                 for c in range(CHUNKS):
                     buf[side, c] = jnp.zeros((rows, width), BF16)
 
-    def direct_rs(c):
-        return relay and c >= DIRECT_RS
-
-    def direct_ag(c):
-        return relay and c >= DIRECT_AG
-
     if relay:
         @pl.when(odd)
         def _():
-            for c in range(DIRECT_RS, CHUNKS):
+            for c in range(ODD_RS):
                 frecv[c, 2] = jnp.zeros(frecv.shape[2:], BF16)
 
     def remote(src, dst, send, recv, to):
@@ -181,7 +175,7 @@
         if relay:
             if i == 2:
                 source, to, recv = mfrecv.at[c, first_axis(h), at], 1 - first_axis(h), mfr_sem.at[c, 1]
-            elif i == first_axis(h):
+            elif i == first_axis(h) and c < ODD_AG:
                 recv = mfl_sem.at[c, h]
         return remote(source, mfrecv.at[c, i, at], mfs_sem.at[c], recv, (peers[to][0], d))
 
@@ -215,7 +209,7 @@
                         region_load[1].wait()
                         far_load[1].wait()
                         pl.semaphore_wait(barrier, greetings)
-            at = pl.ds(i * step, step)
+            at = grid_rows[i]
             em[c, at, :] = silu(mm(gs[at, :], wt[0, :, cols])).astype(BF16)
         far_all = mm(inc[pl.ds(0, long_count)].reshape(long_count * rows, gs.shape[0]), em[c])
         far = [far_all[i * rows:(i + 1) * rows] for i in range(long_count)]
@@ -237,14 +231,13 @@
                     fsend[c, kind, h] = totals[2 if kind == 0 else axis][at].astype(BF16)
                     if kind == 0:
                         fheld[c, h] = totals[1 - axis][at]
-                        if direct_rs(c):
+                        if True:
                             fsend[c, 2, h] = totals[1 - axis][at].astype(BF16)
 
             @pl.when(even)
             def _():
-                if direct_rs(c):
-                    far_direct(c).start()
-                for kind in range(1 if direct_rs(c) else 0, 3 if direct_rs(c) else 2):
+                far_direct(c).start()
+                for kind in (1, 2):
                     for h in range(halves):
                         far_copy(c, h, kind).start()
 
@@ -282,8 +275,13 @@
         def _():
             with scope("rsturn"):
                 pl.semaphore_wait(turn.at[0], 1)
-            for kind in range(2):
-                for c in range(CHUNKS):
+            for c in range(ODD_RS):
+                for h in range(halves):
+                    far_copy(c, h, 0).start()
+            for c in range(ODD_RS, CHUNKS):
+                far_direct(c).start()
+            for c in range(CHUNKS):
+                for kind in (1, 2) if c >= ODD_RS else (1,):
                     for h in range(halves):
                         far_copy(c, h, kind).start()
 
@@ -294,13 +292,8 @@
                 fsend[c, 2, h] = (fheld[c, h] + frelay[c, h].astype(F32)).astype(BF16)
                 far_copy(c, h, 2).start()
 
-        for c in range(CHUNKS):
-            if direct_rs(c):
-                @pl.when(odd)
-                def _():
-                    pass_on(c)
-            else:
-                pass_on(c)
+        for c in range(ODD_RS):
+            pl.when(odd)(functools.partial(pass_on, c))
 
     for loads in late:
         loads[1].wait()
@@ -317,7 +310,8 @@
             dn[k, at, :] = dn[k, at, :] * live[1, k, t].astype(F32).astype(BF16)
 
     def node_update(residual, summed, first, second):
-        hidden = silu(mm(layer_norm(summed).astype(BF16), wt[first])).astype(BF16)
+        cent, half = centred(summed)
+        hidden = gate(half * mm(cent, wt[first])).astype(BF16)
         return (residual.astype(F32) + mm(hidden, wt[second])).astype(BF16)
 
     with scope("nearwait"):
@@ -328,9 +322,9 @@
         total = own_near[:, pl.ds(c * width, width)].astype(F32)
         for s in range(2):
             total = total + nrecv[s, c].astype(F32)
-        slots = 3 if direct_rs(c) else 2 if relay else far_count
+        slots = far_count
         with scope("farwait"):
-            if direct_rs(c):
+            if relay and c < ODD_RS:
                 @pl.when(even)
                 def _():
                     whole(frecv.at[c], fr_sem.at[c], fr_sem.at[c]).wait_recv()
@@ -358,8 +352,7 @@
         else:
             @pl.when(even)
             def _():
-                if direct_ag(c):
-                    mfar_direct(c).start()
+                mfar_direct(c).start()
                 for h in range(halves):
                     mfar_copy(c, h, first_axis(h)).start()
                     mfar_copy(c, h, 1 - first_axis(h)).start()
@@ -378,6 +371,8 @@
             for c in range(CHUNKS):
                 for h in range(halves):
                     mfar_copy(c, h, first_axis(h)).start()
+            for c in range(ODD_AG, CHUNKS):
+                mfar_direct(c).start()
             send_second()
     parts = [mm(pinc[1], msend[c]) for c in range(CHUNKS)]
     if relay:
@@ -387,15 +382,13 @@
                 whole(mfrecv.at[0], mfs_sem.at[0], mfs_sem.at[0]).wait_send()
             hand_over(1)
     if relay:
-        for c in range(CHUNKS):
+        for c in range(ODD_AG):
             for h in range(halves):
                 with scope("mrelaywait"):
                     mfar_copy(c, h, first_axis(h)).wait_recv()
-                if direct_ag(c):
-                    @pl.when(odd)
-                    def _():
-                        mfar_copy(c, h, 2).start()
-                else:
+
+                @pl.when(odd)
+                def _():
                     mfar_copy(c, h, 2).start()
     for s in range(2):
         with scope("mnearwait"):
@@ -405,7 +398,8 @@
     for c in range(CHUNKS):
         with scope("mfarwait"):
             if relay:
-                whole(mfrecv.at[c, 0], mfr_sem.at[c, 0], mfr_sem.at[c, 0]).wait_recv()
+                own = mfrecv.at[c, 0] if c < ODD_AG else mfrecv.at[c, pl.ds(0, 2)]
+                whole(own, mfr_sem.at[c, 0], mfr_sem.at[c, 0]).wait_recv()
             else:
                 whole(mfrecv.at[c], mfr_sem.at[c, 0], mfr_sem.at[c, 0]).wait_recv()
         for i in range(2 if relay else far_count):
@@ -434,14 +428,16 @@
     with scope("ownpart"):
         for c in range(CHUNKS):
             decode(False, c, 1, dsend[c])
-    for s in (near_side, 1 - near_side):
+    for s in (near_side, far_side):
         there = jnp.where(s == 0, not_first, not_last)
         for c in range(CHUNKS):
             with scope("decwait"):
                 @pl.when(there)
                 def _():
                     whole(dnrecv.at[s, c], dr_sem.at[s, c], dr_sem.at[s, c]).wait_recv()
-            decode(True, c, 2 * s, dnrecv[s, c])
+            if s is near_side or c < CHUNKS - 1:
+                decode(True, c, 2 * s, dnrecv[s, c])
+    last[...] = dnrecv[far_side, CHUNKS - 1]
 
     with scope("drain"):
         def far_sent(c):
@@ -461,16 +457,19 @@
                 whole(dsend, ds_sem.at[s], ds_sem.at[s]).wait_send()
 
 
-def finish(mesh_v, gs, dw, acc, grid_o, mesh_o, grid_out, out_sem):
+def finish(mesh_v, gs, dw, acc, dn, last, grid_o, mesh_o, grid_out, out_sem):
     step = gs.shape[0] // (out_sem.shape[0] - 1)
     width = gs.shape[1] // CHUNKS
+    side = lax.rem(lax.axis_index("dev"), 2)
     mesh_copy = pltpu.make_async_copy(mesh_v, mesh_o, out_sem.at[0])
     mesh_copy.start()
     outs = []
     for i in range(gs.shape[0] // step):
         at = pl.ds(i * step, step)
-        normed = layer_norm(acc[at, :]).astype(BF16)
-        parts = [silu(mm(normed, dw[0, :, pl.ds(c * width, width)])).astype(BF16) for c in range(CHUNKS)]
+        held = [acc[at, pl.ds(c * width, width)] for c in range(CHUNKS)]
+        held[-1] = held[-1] + mm(dn[2 * side, at, :], last[...])
+        cent, half = centred(jnp.concatenate(held, axis=1))
+        parts = [gate(half * mm(cent, dw[0, :, pl.ds(c * width, width)])).astype(BF16) for c in range(CHUNKS)]
         hidden = jnp.concatenate(parts, axis=1)
         for c in range(CHUNKS):
             cols = pl.ds(c * width, width)
@@ -506,7 +505,7 @@
     scratch = [
         vmem(rows, feats), vmem(7, feats, feats), vmem(3 + long_count, rows, grid_rows),
         pltpu.SMEM((2, *encode_live.shape), jnp.int32), pltpu.SMEM((2, *encode_groups.shape), jnp.int32),
-        vmem(3 + long_count, rows, rows), vmem(*decode_near.shape),
+        vmem(3 + long_count, rows, rows),
         vmem(CHUNKS, grid_rows, width),
         vmem(CHUNKS, halves, *piece, dtype=F32), vmem(CHUNKS, far_count, halves, *piece),
         vmem(CHUNKS, halves, *piece), vmem(CHUNKS, far_count, halves, *piece),
@@ -514,8 +513,8 @@
         vmem(CHUNKS, *block), vmem(CHUNKS, far_count, *block), vmem(2, CHUNKS, *block),
         vmem(CHUNKS, *block), vmem(2, CHUNKS, *block),
         vmem(rows, feats), vmem(far_count, rows, rows),
-        dma((11,)), dma((GRID_LOADS,)), dma((CHUNKS,)), dma((CHUNKS, halves)), dma((CHUNKS,)), dma((2,)), dma((2,)),
-        dma((CHUNKS,)), dma((CHUNKS, halves)), dma((CHUNKS, halves)), dma((2,)), dma((2,)), dma((2,)), dma((2, CHUNKS)), pltpu.SemaphoreType.REGULAR((2,)),
+        dma((10,)), dma((2,)), dma((CHUNKS,)), dma((ODD_RS, halves)), dma((CHUNKS,)), dma((2,)), dma((2,)),
+        dma((CHUNKS,)), dma((ODD_AG, halves)), dma((CHUNKS, 2)), dma((2,)), dma((2,)), dma((2,)), dma((2, CHUNKS)), pltpu.SemaphoreType.REGULAR((2,)),
     ]
     hbm = pl.BlockSpec(memory_space=pltpu.HBM)
     on_chip = pl.BlockSpec(memory_space=pltpu.VMEM)
@@ -523,9 +522,10 @@
         functools.partial(exchange, groups, devs),
         out_shape=(
             vmem(*mesh_state.shape), vmem(*grid_state.shape), vmem(2, feats, feats), vmem(*grid_state.shape, dtype=F32),
+            vmem(*decode_near.shape), vmem(*block),
         ),
         in_specs=[hbm] * len(args),
-        out_specs=(on_chip,) * 4,
+        out_specs=(on_chip,) * 6,
         scratch_shapes=scratch,
         compiler_params=pltpu.CompilerParams(collective_id=0, has_side_effects=True, vmem_limit_bytes=32 << 20),
         name="exchange",
@@ -536,7 +536,7 @@
             jax.ShapeDtypeStruct(grid_state.shape, BF16),
             jax.ShapeDtypeStruct(mesh_state.shape, BF16),
         ),
-        in_specs=[on_chip] * 4,
+        in_specs=[on_chip] * 6,
         out_specs=(hbm, hbm),
         scratch_shapes=[vmem(*grid_state.shape), dma((1 + GRID_OUTS,))],
         compiler_params=pltpu.CompilerParams(vmem_limit_bytes=16 << 20),

time: 26.5 us -> 25.8 us (0.974)
  Pallas kernels: 25.7 us -> 25 us
    pallas_call x1, Pallas kernels: 23.1 us -> 22.4 us  [body(): pl.pallas_call(functools.partial(exchange, groups, devs), out_shape=(vmem...]
where the time goes in v4:
time: 25.8 us; the launch traced here: 25.7 us
  Pallas kernels  25 us (97%)
  between operations  0.65 us (3%)
    pallas_call x1, Pallas kernels, body(): pl.pallas_call(functools.partial(exchange, groups, devs), out_shape=(vmem...  22.4 us
    pallas_call x1, Pallas kernels, body(): pl.pallas_call(finish, out_shape=(jax.ShapeDtypeStruct(grid_state.shape,...  2.6 us

profile of v4, /device:TPU:1, one launch (start us, length us, event | category | flops | bytes accessed | tf_op | source)
XLA Modules:
  0.0 25.7 jit_solution(10110669440977880102)
XLA Ops:
  0.6 22.4 %exchange.1 = (bf16[128,512]{1,0:T(8,128)(2,1)S(1)}, bf16[1024,512]{1,0:T(8,128)(2,1)S(1)}, bf16[2,512,512]{2,1,0:T(8,128)(2,1)S(1)}, f32[1024,512]{1,0:T(8,128)...) custom-call(bf16[1024,512]{1,0:T(8,128)(2,1)} %grid_h.1, bf16[128,512]{1,0:T(8,128)(2,1)} %mesh_h.1, ...), custom_call_target="tpu_custom_call" | custom-call | tf_op jit(solution)/shard_map/exchange/pallas_call | solution.py:521
  23.1 2.6 %finish.1 = (bf16[1024,512]{1,0:T(8,128)(2,1)}, bf16[128,512]{1,0:T(8,128)(2,1)}) custom-call(bf16[128,512]{1,0:T(8,128)(2,1)S(1)} %get-tuple-element.8.mesh_v, bf16[1024,512]{1,0:T(8,128)(2,1)S(1)} %get-tuple-element.9.gs, bf16[2,512,512]{2,1,0:T(8,128)(2,1)S(1)} %get-tuple-element.10.dw, f32[1024,512]{1,0:T(8,128)S(1)} %get-tuple-element.11.acc, ...), custom_call_target="tpu_custom_call" | custom-call | tf_op jit(solution)/shard_map/finish/pallas_call | solution.py:533

commit v5 on v4

--- a/solution.py
+++ b/solution.py
@@ -161,7 +161,7 @@
         return remote(fsend.at[c, kind, h], frecv.at[c, kind - 1, h], fs_sem.at[c], fr_sem.at[c], (peers[to][0], d))
 
     def far_direct(c):
-        return remote(fsend.at[c, 0], frecv.at[c, 2], fs_sem.at[c], fr_sem.at[c], (peers[2][0], d))
+        return remote(fsend.at[c, 0], frecv.at[c, 2], fs_sem.at[CHUNKS if c else 0], fr_sem.at[c], (peers[2][0], d))
 
     def mfar_direct(c):
         return remote(msend.at[c], mfrecv.at[c, 2], mfs_sem.at[c], mfr_sem.at[c, 1], (peers[2][0], d))
@@ -269,6 +269,7 @@
         def _():
             with scope("rsdrain"):
                 whole(fsend.at[0], fs_sem.at[0], fs_sem.at[0]).wait_send()
+                whole(fsend.at[1, 0], fs_sem.at[CHUNKS], fs_sem.at[CHUNKS]).wait_send()
             hand_over(0)
 
         @pl.when(odd)
@@ -368,12 +369,14 @@
         def _():
             with scope("oddwait"):
                 pl.semaphore_wait(turn.at[1], 1)
-            for c in range(CHUNKS):
-                for h in range(halves):
-                    mfar_copy(c, h, first_axis(h)).start()
+            for h in range(halves):
+                mfar_copy(0, h, first_axis(h)).start()
             for c in range(ODD_AG, CHUNKS):
                 mfar_direct(c).start()
-            send_second()
+            for h in range(halves):
+                mfar_copy(1, h, first_axis(h)).start()
+            for h in range(halves):
+                mfar_copy(0, h, 1 - first_axis(h)).start()
     parts = [mm(pinc[1], msend[c]) for c in range(CHUNKS)]
     if relay:
         @pl.when(even)
@@ -390,6 +393,11 @@
                 @pl.when(odd)
                 def _():
                     mfar_copy(c, h, 2).start()
+
+        @pl.when(odd)
+        def _():
+            for h in range(halves):
+                mfar_copy(1, h, 1 - first_axis(h)).start()
     for s in range(2):
         with scope("mnearwait"):
             wait_side(mnrecv, mnr_sem, s)
@@ -441,8 +449,11 @@
 
     with scope("drain"):
         def far_sent(c):
-            whole(fsend.at[c], fs_sem.at[c], fs_sem.at[c]).wait_send()
+            sent = fsend.at[c, pl.ds(1, 2)] if relay and c else fsend.at[c]
+            whole(sent, fs_sem.at[c], fs_sem.at[c]).wait_send()
             whole(mfrecv.at[c], mfs_sem.at[c], mfs_sem.at[c]).wait_send()
+            if relay and c == 0:
+                whole(fsend.at[1, 0], fs_sem.at[CHUNKS], fs_sem.at[CHUNKS]).wait_send()
 
         for c in range(CHUNKS):
             if relay and c == 0:
@@ -513,7 +524,7 @@
         vmem(CHUNKS, *block), vmem(CHUNKS, far_count, *block), vmem(2, CHUNKS, *block),
         vmem(CHUNKS, *block), vmem(2, CHUNKS, *block),
         vmem(rows, feats), vmem(far_count, rows, rows),
-        dma((10,)), dma((2,)), dma((CHUNKS,)), dma((ODD_RS, halves)), dma((CHUNKS,)), dma((2,)), dma((2,)),
+        dma((10,)), dma((2,)), dma((CHUNKS + 1,)), dma((ODD_RS, halves)), dma((CHUNKS,)), dma((2,)), dma((2,)),
         dma((CHUNKS,)), dma((ODD_AG, halves)), dma((CHUNKS, 2)), dma((2,)), dma((2,)), dma((2,)), dma((2, CHUNKS)), pltpu.SemaphoreType.REGULAR((2,)),
     ]
     hbm = pl.BlockSpec(memory_space=pltpu.HBM)

time: 25.8 us -> 25.4 us (0.984)
  Pallas kernels: 25 us -> 24.6 us
    pallas_call x1, Pallas kernels: 22.4 us -> 22 us  [body(): pl.pallas_call(functools.partial(exchange, groups, devs), out_shape=(vmem...]
where the time goes in v5:
time: 25.4 us; the launch traced here: 25.2 us
  Pallas kernels  24.6 us (97%)
  between operations  0.65 us (3%)
    pallas_call x1, Pallas kernels, body(): pl.pallas_call(functools.partial(exchange, groups, devs), out_shape=(vmem...  22 us
    pallas_call x1, Pallas kernels, body(): pl.pallas_call(finish, out_shape=(jax.ShapeDtypeStruct(grid_state.shape,...  2.6 us

profile of v5, /device:TPU:1, one launch (start us, length us, event | category | flops | bytes accessed | tf_op | source)
XLA Modules:
  0.0 25.2 jit_solution(7387667328217611679)
XLA Ops:
  0.6 22.0 %exchange.1 = (bf16[128,512]{1,0:T(8,128)(2,1)S(1)}, bf16[1024,512]{1,0:T(8,128)(2,1)S(1)}, bf16[2,512,512]{2,1,0:T(8,128)(2,1)S(1)}, f32[1024,512]{1,0:T(8,128)...) custom-call(bf16[1024,512]{1,0:T(8,128)(2,1)} %grid_h.1, bf16[128,512]{1,0:T(8,128)(2,1)} %mesh_h.1, ...), custom_call_target="tpu_custom_call" | custom-call | tf_op jit(solution)/shard_map/exchange/pallas_call | solution.py:532
  22.6 2.6 %finish.1 = (bf16[1024,512]{1,0:T(8,128)(2,1)}, bf16[128,512]{1,0:T(8,128)(2,1)}) custom-call(bf16[128,512]{1,0:T(8,128)(2,1)S(1)} %get-tuple-element.8.mesh_v, bf16[1024,512]{1,0:T(8,128)(2,1)S(1)} %get-tuple-element.9.gs, bf16[2,512,512]{2,1,0:T(8,128)(2,1)S(1)} %get-tuple-element.10.dw, f32[1024,512]{1,0:T(8,128)S(1)} %get-tuple-element.11.acc, ...), custom_call_target="tpu_custom_call" | custom-call | tf_op jit(solution)/shard_map/finish/pallas_call | solution.py:544

commit v6 on v5

--- a/solution.py
+++ b/solution.py
@@ -55,8 +55,8 @@
     devs,
     grid_h, mesh_h, ee_h, e1_h, e2_h, pe_h, p1_h, p2_h, de_h, d1_h, d2_h,
     en_h, el_h, ef_h, eg_h, pn_h, pf_h, pg_h, dn_h, dl_h,
-    mesh_out, gs, dw, acc, dn, last,
-    ms, wt, inc, live, regions, pinc,
+    mesh_out, gs, dw, acc,
+    ms, wt, inc, live, regions, pinc, dn,
     em, fheld, fsend, frelay, frecv, nsend, nrecv, msend, mfrecv, mnrecv, dsend, dnrecv,
     own_near, proc_inc,
     load_sem, grid_sem, fs_sem, fl_sem, fr_sem, ns_sem, nr_sem, mfs_sem, mfl_sem, mfr_sem, mns_sem, mnr_sem, ds_sem, dr_sem, turn,
@@ -164,7 +164,7 @@
         return remote(fsend.at[c, 0], frecv.at[c, 2], fs_sem.at[CHUNKS if c else 0], fr_sem.at[c], (peers[2][0], d))
 
     def mfar_direct(c):
-        return remote(msend.at[c], mfrecv.at[c, 2], mfs_sem.at[c], mfr_sem.at[c, 1], (peers[2][0], d))
+        return remote(msend.at[c], mfrecv.at[c, 2], mfs_sem.at[CHUNKS if c else 0], mfr_sem.at[c, 1], (peers[2][0], d))
 
     def near_copy(c, s):
         return remote(nsend.at[s, c], nrecv.at[1 - s, c], ns_sem.at[s], nr_sem.at[1 - s], (g, sides[s][1]))
@@ -383,6 +383,7 @@
         def _():
             with scope("agdrain"):
                 whole(mfrecv.at[0], mfs_sem.at[0], mfs_sem.at[0]).wait_send()
+                whole(msend.at[1], mfs_sem.at[CHUNKS], mfs_sem.at[CHUNKS]).wait_send()
             hand_over(1)
     if relay:
         for c in range(ODD_AG):
@@ -443,16 +444,16 @@
                 @pl.when(there)
                 def _():
                     whole(dnrecv.at[s, c], dr_sem.at[s, c], dr_sem.at[s, c]).wait_recv()
-            if s is near_side or c < CHUNKS - 1:
-                decode(True, c, 2 * s, dnrecv[s, c])
-    last[...] = dnrecv[far_side, CHUNKS - 1]
+            decode(True, c, 2 * s, dnrecv[s, c])
 
     with scope("drain"):
         def far_sent(c):
             sent = fsend.at[c, pl.ds(1, 2)] if relay and c else fsend.at[c]
             whole(sent, fs_sem.at[c], fs_sem.at[c]).wait_send()
-            whole(mfrecv.at[c], mfs_sem.at[c], mfs_sem.at[c]).wait_send()
+            sent = mfrecv.at[c, pl.ds(0, 2)] if relay and c else mfrecv.at[c]
+            whole(sent, mfs_sem.at[c], mfs_sem.at[c]).wait_send()
             if relay and c == 0:
+                whole(msend.at[1], mfs_sem.at[CHUNKS], mfs_sem.at[CHUNKS]).wait_send()
                 whole(fsend.at[1, 0], fs_sem.at[CHUNKS], fs_sem.at[CHUNKS]).wait_send()
 
         for c in range(CHUNKS):
@@ -468,17 +469,15 @@
                 whole(dsend, ds_sem.at[s], ds_sem.at[s]).wait_send()
 
 
-def finish(mesh_v, gs, dw, acc, dn, last, grid_o, mesh_o, grid_out, out_sem):
+def finish(mesh_v, gs, dw, acc, grid_o, mesh_o, grid_out, out_sem):
     step = gs.shape[0] // (out_sem.shape[0] - 1)
     width = gs.shape[1] // CHUNKS
-    side = lax.rem(lax.axis_index("dev"), 2)
     mesh_copy = pltpu.make_async_copy(mesh_v, mesh_o, out_sem.at[0])
     mesh_copy.start()
     outs = []
     for i in range(gs.shape[0] // step):
         at = pl.ds(i * step, step)
         held = [acc[at, pl.ds(c * width, width)] for c in range(CHUNKS)]
-        held[-1] = held[-1] + mm(dn[2 * side, at, :], last[...])
         cent, half = centred(jnp.concatenate(held, axis=1))
         parts = [gate(half * mm(cent, dw[0, :, pl.ds(c * width, width)])).astype(BF16) for c in range(CHUNKS)]
         hidden = jnp.concatenate(parts, axis=1)
@@ -516,7 +515,7 @@
     scratch = [
         vmem(rows, feats), vmem(7, feats, feats), vmem(3 + long_count, rows, grid_rows),
         pltpu.SMEM((2, *encode_live.shape), jnp.int32), pltpu.SMEM((2, *encode_groups.shape), jnp.int32),
-        vmem(3 + long_count, rows, rows),
+        vmem(3 + long_count, rows, rows), vmem(*decode_near.shape),
         vmem(CHUNKS, grid_rows, width),
         vmem(CHUNKS, halves, *piece, dtype=F32), vmem(CHUNKS, far_count, halves, *piece),
         vmem(CHUNKS, halves, *piece), vmem(CHUNKS, far_count, halves, *piece),
@@ -525,7 +524,7 @@
         vmem(CHUNKS, *block), vmem(2, CHUNKS, *block),
         vmem(rows, feats), vmem(far_count, rows, rows),
         dma((10,)), dma((2,)), dma((CHUNKS + 1,)), dma((ODD_RS, halves)), dma((CHUNKS,)), dma((2,)), dma((2,)),
-        dma((CHUNKS,)), dma((ODD_AG, halves)), dma((CHUNKS, 2)), dma((2,)), dma((2,)), dma((2,)), dma((2, CHUNKS)), pltpu.SemaphoreType.REGULAR((2,)),
+        dma((CHUNKS + 1,)), dma((ODD_AG, halves)), dma((CHUNKS, 2)), dma((2,)), dma((2,)), dma((2,)), dma((2, CHUNKS)), pltpu.SemaphoreType.REGULAR((2,)),
     ]
     hbm = pl.BlockSpec(memory_space=pltpu.HBM)
     on_chip = pl.BlockSpec(memory_space=pltpu.VMEM)
@@ -533,10 +532,9 @@
         functools.partial(exchange, groups, devs),
         out_shape=(
             vmem(*mesh_state.shape), vmem(*grid_state.shape), vmem(2, feats, feats), vmem(*grid_state.shape, dtype=F32),
-            vmem(*decode_near.shape), vmem(*block),
         ),
         in_specs=[hbm] * len(args),
-        out_specs=(on_chip,) * 6,
+        out_specs=(on_chip,) * 4,
         scratch_shapes=scratch,
         compiler_params=pltpu.CompilerParams(collective_id=0, has_side_effects=True, vmem_limit_bytes=32 << 20),
         name="exchange",
@@ -547,7 +545,7 @@
             jax.ShapeDtypeStruct(grid_state.shape, BF16),
             jax.ShapeDtypeStruct(mesh_state.shape, BF16),
         ),
-        in_specs=[on_chip] * 6,
+        in_specs=[on_chip] * 4,
         out_specs=(hbm, hbm),
         scratch_shapes=[vmem(*grid_state.shape), dma((1 + GRID_OUTS,))],
         compiler_params=pltpu.CompilerParams(vmem_limit_bytes=16 << 20),

time: 25.4 us -> 24.9 us (0.980)
  Pallas kernels: 24.6 us -> 24.1 us
    pallas_call x1, Pallas kernels: 2.6 us -> 2.25 us  [body(): pl.pallas_call(finish, out_shape=(jax.ShapeDtypeStruct(grid_state.shape,...]
where the time goes in v6:
time: 24.9 us; the launch traced here: 24.7 us
  Pallas kernels  24.1 us (97%)
  between operations  0.65 us (3%)
    pallas_call x1, Pallas kernels, body(): pl.pallas_call(functools.partial(exchange, groups, devs), out_shape=(vmem...  21.8 us
    pallas_call x1, Pallas kernels, body(): pl.pallas_call(finish, out_shape=(jax.ShapeDtypeStruct(grid_state.shape,...  2.25 us

profile of v6, /device:TPU:1, one launch (start us, length us, event | category | flops | bytes accessed | tf_op | source)
XLA Modules:
  0.0 24.7 jit_solution(15169027819956285992)
XLA Ops:
  0.6 21.8 %exchange.1 = (bf16[128,512]{1,0:T(8,128)(2,1)S(1)}, bf16[1024,512]{1,0:T(8,128)(2,1)S(1)}, bf16[2,512,512]{2,1,0:T(8,128)(2,1)S(1)}, f32[1024,512]{1,0:T(8,128)S(1)}) custom-call(bf16[1024,512]{1,0:T(8,128)(2,1)} %grid_h.1, bf16[128,512]{1,0:T(8,128)(2,1)} %mesh_h.1, bf16[512,512]{1,0:T(8,128)(2,1)} %ee_h.1, bf16[512,512]{1,0:T(8,128)(2,1)} %e1_h.1, ...), custom_call_target="tpu_custom_call" | custom-call | tf_op jit(solution)/shard_map/exchange/pallas_call | solution.py:531
  22.5 2.2 %finish.1 = (bf16[1024,512]{1,0:T(8,128)(2,1)}, bf16[128,512]{1,0:T(8,128)(2,1)}) custom-call(bf16[128,512]{1,0:T(8,128)(2,1)S(1)} %get-tuple-element.6.mesh_v, bf16[1024,512]{1,0:T(8,128)(2,1)S(1)} %get-tuple-element.7.gs, bf16[2,512,512]{2,1,0:T(8,128)(2,1)S(1)} %get-tuple-element.8.dw, f32[1024,512]{1,0:T(8,128)S(1)} %get-tuple-element.9.acc), custom_call_target="tpu_custom_call" | custom-call | tf_op jit(solution)/shard_map/finish/pallas_call | solution.py:542
